TPU v7x, 768 devices: a whole 4x8x12 slice. The times are simulated.
768 devices in a mesh: row: 12 (over z), col: 64 (over y, x, core).
Axes of the slice: x: 4, y: 8, z: 12, core: 2. Of those that a mesh axis runs over, the one named last changes fastest.
Arguments:
- positions: float32 [3, 12582912], P(None, ('row', 'col')), may hold values from 0 to 1
- masses: float32 [1, 12582912], P(None, ('row', 'col')), may hold values from 2e-09 to 2e-08
- counts: int32 [1, 98304], P(None, ('row', 'col')), may hold values from 32 to 128
- sources: int32 [98304, 8], P(('row', 'col')), may hold values from 0 to 383, as said below
Outputs:
- accel: float32 [3, 12582912], P(None, ('row', 'col'))
Inputs may be any that keep to these rules, and one draw needn't show every extreme that they name: `sources`: each device's source ids name exactly 32 distinct leaves of the lower row neighbour and exactly 32 of the upper one.
All inputs are finite; a program needn't handle non-finite values.
Results may differ from a plain program's by a relative error of at most 0.00024.
Values sent between devices are 32-bit elements; how exact they have to be, the bound alone decides.
No kernel may reach another device: no remote copies, remote signals or barrier semaphores. Data moves between devices by JAX's collectives and lax.ppermute only.
A program may use at most 32 MiB of HBM per device.

v0:
```python
import jax
import jax.numpy as jnp
from jax import lax
from jax.sharding import PartitionSpec as P

softening = 2.5e-07


def sent_together(arrays, axis, split_dim, concat_dim, along):
    ends, at = ([], 0)
    for a in arrays[:-1]:
        at += a.shape[along]
        ends.append(at)
    both = jnp.concatenate(arrays, axis=along)
    return tuple(
        jnp.split(
            lax.all_to_all(both, axis, split_axis=split_dim, concat_axis=concat_dim, tiled=True),
            ends,
            axis=along,
        )
    )


def padded_2(shard, sides, width):
    for axis, dim in sides:
        size, length = (lax.axis_size(axis), shard.shape[dim])
        up = [(i, (i + 1) % size) for i in range(size)]
        down = [(j, i) for i, j in up]
        last = lax.slice_in_dim(shard, length - width, length, axis=dim)
        leading = lax.slice_in_dim(shard, 0, width, axis=dim)
        before = lax.ppermute(last, axis, up)
        after = lax.ppermute(leading, axis, down)
        shard = jnp.concatenate([before, shard, after], axis=dim)
    return shard


def leaf_forces(full_table, targets, sources, alive):
    count = targets.shape[0]
    width = targets.shape[2]
    target_groups = targets.reshape(count // 8, 8, 4, width)
    source_groups = sources.reshape(count // 8, 8, sources.shape[1])
    alive_groups = alive.reshape(count // 8, 8, width)

    def one_group(items):
        target, index, living = items
        source = full_table[index]
        delta_x = source[:, :, 0, None, :] - target[:, None, 0, :, None]
        delta_y = source[:, :, 1, None, :] - target[:, None, 1, :, None]
        delta_z = source[:, :, 2, None, :] - target[:, None, 2, :, None]
        spread = softening + delta_x * delta_x + delta_y * delta_y + delta_z * delta_z
        weight = source[:, :, 3, None, :] / (spread * jnp.sqrt(spread))
        pull_x = jnp.sum(weight * delta_x, axis=(1, 3))
        pull_y = jnp.sum(weight * delta_y, axis=(1, 3))
        pull_z = jnp.sum(weight * delta_z, axis=(1, 3))
        return jnp.stack([pull_x, pull_y, pull_z], axis=1) * living[:, None, :]

    out = lax.map(one_group, (target_groups, source_groups, alive_groups))
    return out.reshape(count, 3, width)


def on_device(positions, masses, counts, sources):
    coords, weights, livecount = (
        *sent_together((positions, masses), "col", 1, 1, 0),
        lax.all_to_all(counts, "col", split_axis=1, concat_axis=1, tiled=True),
    )
    leaves = livecount.shape[1]
    width = coords.shape[1] // leaves
    alive = (
        lax.broadcasted_iota(jnp.int32, (leaves, width), 1) < livecount.reshape(leaves, 1)
    ).astype(jnp.float32)
    table = jnp.concatenate(
        [coords.reshape(3, leaves, width), (weights.reshape(leaves, width) * alive)[None]], axis=0
    )
    table = table.transpose(1, 0, 2)
    padded = padded_2(table, (("row", 0),), leaves)
    full = jnp.concatenate(
        [padded[leaves : 2 * leaves], padded[:leaves], padded[2 * leaves :]], axis=0
    )
    result = leaf_forces(full, table, sources, alive)
    return result.transpose(1, 0, 2).reshape(3, leaves * width)


def solution(mesh):
    return jax.shard_map(
        on_device,
        mesh=mesh,
        in_specs=(
            P(None, ("row", "col")),
            P(None, ("row", "col")),
            P(None, ("row", "col")),
            P(("row", "col"), None),
        ),
        out_specs=P(None, ("row", "col")),
        check_vma=False,
    )
```

profile of v0, /device:TPU:1, one launch (start us, length us, event | category | flops | bytes accessed | tf_op | source)
XLA Modules:
  0.0 144.2 jit_solution(18073762593138448461)
XLA Ops:
  0.0 0.6 broadcast.80
  0.6 1.3 reduce.8
  1.9 0.7 all_to_all.14
  2.6 14.5 %all-to-all-start.1 = ((s32[1,64,2]{2,0,1:T(1,128)}), s32[1,64,2]{2,0,1:T(1,128)S(1)}, u32[]{:S(2)}, u32[]{:S(2)}) async-start(s32[1,64,2]{2,0,1:T(1,128)} %bitcast.16), calls=%async_computation.1 | async-start | bytes 65536 | tf_op jit(solution)/shard_map/all_to_all | solution.py:64
  17.2 1.8 %pad_maximum_fusion.1 = f32[4,16384]{1,0:T(4,128)} fusion(f32[1,16384]{1,0:T(1,128)} %param.7, f32[3,16384]{1,0:T(4,128)} %param.6), kind=kLoop, calls=%fused_computation.27 | loop fusion | flops 65536 | bytes 524288 | tf_op jit(solution)/shard_map/concatenate | solution.py:14
  19.0 7.7 %all-to-all-done.1 = s32[1,64,2]{2,0,1:T(1,128)S(1)} async-done(((s32[1,64,2]{2,0,1:T(1,128)}), s32[1,64,2]{2,0,1:T(1,128)S(1)}, u32[]{:S(2)}, u32[]{:S(2)}) %all-to-all-start.1) | async-done | bytes 544 | tf_op jit(solution)/shard_map/all_to_all | solution.py:64
  26.7 4.7 %all-to-all-start = ((f32[4,64,256]{2,0,1:T(4,128)}), f32[4,64,256]{2,0,1:T(4,128)S(1)}, u32[]{:S(2)}, u32[]{:S(2)}) async-start(f32[4,64,256]{2,0,1:T(4,128)} %bitcast.15), calls=%async_computation | async-start | bytes 524288 | tf_op jit(solution)/shard_map/all_to_all | solution.py:17
  31.4 0.7 reduce.9
  32.1 0.1 lt.37
  32.2 12.3 %all-to-all-done = f32[4,64,256]{2,0,1:T(4,128)S(1)} async-done(((f32[4,64,256]{2,0,1:T(4,128)}), f32[4,64,256]{2,0,1:T(4,128)S(1)}, u32[]{:S(2)}, u32[]{:S(2)}) %all-to-all-start) | async-done | bytes 262176 | tf_op jit(solution)/shard_map/all_to_all | solution.py:17
  44.8 1.9 %collective-permute-start = (f32[128,4,128]{2,0,1:T(8,128)S(1)}, f32[128,4,128]{2,0,1:T(8,128)S(1)}, u32[]{:S(2)}, u32[]{:S(2)}) collective-permute-start(f32[128,4,128]{2,0,1:T(8,128)S(1)} %get-tuple-element.85), channel_id=1, source_target_pairs={{0,64},{64,128},{128,192},{192,256},{256,320},{320,384},{384,448},... | collective-permute-start | bytes 786440 | tf_op jit(solution)/shard_map/ppermute | solution.py:31
  46.7 11.3 %collective-permute-start.1 = (f32[128,4,128]{2,0,1:T(8,128)S(1)}, f32[128,4,128]{2,0,1:T(8,128)S(1)}, u32[]{:S(2)}, u32[]{:S(2)}) collective-permute-start(f32[128,4,128]{2,0,1:T(8,128)S(1)} %get-tuple-element.85), channel_id=1, source_target_pairs={{64,0},{128,64},{192,128},{256,192},{320,256},{384,320},{448,384},... | collective-permute-start | bytes 786440 | tf_op jit(solution)/shard_map/ppermute | solution.py:32
  58.1 0.1 copy.22
  58.3 4.2 %collective-permute-done = f32[128,4,128]{2,0,1:T(8,128)S(1)} collective-permute-done((f32[128,4,128]{2,0,1:T(8,128)S(1)}, f32[128,4,128]{2,0,1:T(8,128)S(1)}, u32[]{:S(2)}, u32[]{:S(2)}) %collective-permute-start) | collective-permute-done | bytes 262176 | tf_op jit(solution)/shard_map/ppermute | solution.py:31
  62.5 0.9 collective-permute-done.1
  63.5 0.5 copy.25
  64.0 79.3 %while.10 = (s32[]{:T(128)}, f32[16,8,3,128]{3,1,0,2:T(8,128)S(1)}, s32[16,8,8]{2,1,0:T(8,128)S(1)}, f32[384,4,128]{2,1,0:T(4,128)S(1)}, f32[16,8,4,128]{3,1,0,2...) while((s32[]{:T(128)}, f32[16,8,3,128]{3,1,0,2:T(8,128)S(1)}, s32[16,8,8]{2,1,0:T(8,128)S(1)}, ...), condition=%wide.region_4.5_spmd, body=%wide.region_0.4_spmd.sunk | while | flops 17833152 | bytes 779869 | solution.py:57
  64.1 0.7 gather_fusion
  64.8 0.1 fusion.17
  64.9 4.0 %fusion.18 = (f32[8,128]{1,0:T(8,128)S(1)}, f32[8,128]{1,0:T(8,128)S(1)}, f32[8,128]{1,0:T(8,128)S(1)}) fusion(f32[8,128]{1,0:T(8,128)S(1)} %get-tuple-element.133, f32[8,8,128]{2,1,0:T(8,128)S(1)} %bitcast.77, f32[8,128]{1,0:T(8,128)S(1)} %get-tuple-element.135, f32[8,8,128]{2,1,0:T(8,128)S(1)} %bitcast.78, f32[8,128]{1,0:T(8,128)S(1)} %get-tuple-element.137, ...), kind=kLoop, calls=%fused_computation.11.clone.1 | loop fusion | flops 17822720 | bytes 155648 | tf_op jit(solution)/shard_map/while/body/eval_jaxpr/reduce_sum | solution.py:52
  69.1 0.7 gather_fusion
  69.7 0.1 fusion.17
  69.9 4.0 %fusion.18 = (f32[8,128]{1,0:T(8,128)S(1)}, f32[8,128]{1,0:T(8,128)S(1)}, f32[8,128]{1,0:T(8,128)S(1)}) fusion(f32[8,128]{1,0:T(8,128)S(1)} %get-tuple-element.133, f32[8,8,128]{2,1,0:T(8,128)S(1)} %bitcast.77, f32[8,128]{1,0:T(8,128)S(1)} %get-tuple-element.135, f32[8,8,128]{2,1,0:T(8,128)S(1)} %bitcast.78, f32[8,128]{1,0:T(8,128)S(1)} %get-tuple-element.137, ...), kind=kLoop, calls=%fused_computation.11.clone.1 | loop fusion | flops 17822720 | bytes 155648 | tf_op jit(solution)/shard_map/while/body/eval_jaxpr/reduce_sum | solution.py:52
  74.0 0.7 gather_fusion
  74.7 0.1 fusion.17
  74.8 4.0 %fusion.18 = (f32[8,128]{1,0:T(8,128)S(1)}, f32[8,128]{1,0:T(8,128)S(1)}, f32[8,128]{1,0:T(8,128)S(1)}) fusion(f32[8,128]{1,0:T(8,128)S(1)} %get-tuple-element.133, f32[8,8,128]{2,1,0:T(8,128)S(1)} %bitcast.77, f32[8,128]{1,0:T(8,128)S(1)} %get-tuple-element.135, f32[8,8,128]{2,1,0:T(8,128)S(1)} %bitcast.78, f32[8,128]{1,0:T(8,128)S(1)} %get-tuple-element.137, ...), kind=kLoop, calls=%fused_computation.11.clone.1 | loop fusion | flops 17822720 | bytes 155648 | tf_op jit(solution)/shard_map/while/body/eval_jaxpr/reduce_sum | solution.py:52
  79.0 0.7 gather_fusion
  79.6 0.1 fusion.17
  79.8 4.0 %fusion.18 = (f32[8,128]{1,0:T(8,128)S(1)}, f32[8,128]{1,0:T(8,128)S(1)}, f32[8,128]{1,0:T(8,128)S(1)}) fusion(f32[8,128]{1,0:T(8,128)S(1)} %get-tuple-element.133, f32[8,8,128]{2,1,0:T(8,128)S(1)} %bitcast.77, f32[8,128]{1,0:T(8,128)S(1)} %get-tuple-element.135, f32[8,8,128]{2,1,0:T(8,128)S(1)} %bitcast.78, f32[8,128]{1,0:T(8,128)S(1)} %get-tuple-element.137, ...), kind=kLoop, calls=%fused_computation.11.clone.1 | loop fusion | flops 17822720 | bytes 155648 | tf_op jit(solution)/shard_map/while/body/eval_jaxpr/reduce_sum | solution.py:52
  83.9 0.7 gather_fusion
  84.6 0.1 fusion.17
  84.7 4.0 %fusion.18 = (f32[8,128]{1,0:T(8,128)S(1)}, f32[8,128]{1,0:T(8,128)S(1)}, f32[8,128]{1,0:T(8,128)S(1)}) fusion(f32[8,128]{1,0:T(8,128)S(1)} %get-tuple-element.133, f32[8,8,128]{2,1,0:T(8,128)S(1)} %bitcast.77, f32[8,128]{1,0:T(8,128)S(1)} %get-tuple-element.135, f32[8,8,128]{2,1,0:T(8,128)S(1)} %bitcast.78, f32[8,128]{1,0:T(8,128)S(1)} %get-tuple-element.137, ...), kind=kLoop, calls=%fused_computation.11.clone.1 | loop fusion | flops 17822720 | bytes 155648 | tf_op jit(solution)/shard_map/while/body/eval_jaxpr/reduce_sum | solution.py:52
  88.9 0.7 gather_fusion
  89.6 0.1 fusion.17
  89.7 4.0 %fusion.18 = (f32[8,128]{1,0:T(8,128)S(1)}, f32[8,128]{1,0:T(8,128)S(1)}, f32[8,128]{1,0:T(8,128)S(1)}) fusion(f32[8,128]{1,0:T(8,128)S(1)} %get-tuple-element.133, f32[8,8,128]{2,1,0:T(8,128)S(1)} %bitcast.77, f32[8,128]{1,0:T(8,128)S(1)} %get-tuple-element.135, f32[8,8,128]{2,1,0:T(8,128)S(1)} %bitcast.78, f32[8,128]{1,0:T(8,128)S(1)} %get-tuple-element.137, ...), kind=kLoop, calls=%fused_computation.11.clone.1 | loop fusion | flops 17822720 | bytes 155648 | tf_op jit(solution)/shard_map/while/body/eval_jaxpr/reduce_sum | solution.py:52
  93.9 0.7 gather_fusion
  94.5 0.1 fusion.17
  94.6 4.0 %fusion.18 = (f32[8,128]{1,0:T(8,128)S(1)}, f32[8,128]{1,0:T(8,128)S(1)}, f32[8,128]{1,0:T(8,128)S(1)}) fusion(f32[8,128]{1,0:T(8,128)S(1)} %get-tuple-element.133, f32[8,8,128]{2,1,0:T(8,128)S(1)} %bitcast.77, f32[8,128]{1,0:T(8,128)S(1)} %get-tuple-element.135, f32[8,8,128]{2,1,0:T(8,128)S(1)} %bitcast.78, f32[8,128]{1,0:T(8,128)S(1)} %get-tuple-element.137, ...), kind=kLoop, calls=%fused_computation.11.clone.1 | loop fusion | flops 17822720 | bytes 155648 | tf_op jit(solution)/shard_map/while/body/eval_jaxpr/reduce_sum | solution.py:52
  98.8 0.7 gather_fusion
  99.5 0.1 fusion.17
  99.6 4.0 %fusion.18 = (f32[8,128]{1,0:T(8,128)S(1)}, f32[8,128]{1,0:T(8,128)S(1)}, f32[8,128]{1,0:T(8,128)S(1)}) fusion(f32[8,128]{1,0:T(8,128)S(1)} %get-tuple-element.133, f32[8,8,128]{2,1,0:T(8,128)S(1)} %bitcast.77, f32[8,128]{1,0:T(8,128)S(1)} %get-tuple-element.135, f32[8,8,128]{2,1,0:T(8,128)S(1)} %bitcast.78, f32[8,128]{1,0:T(8,128)S(1)} %get-tuple-element.137, ...), kind=kLoop, calls=%fused_computation.11.clone.1 | loop fusion | flops 17822720 | bytes 155648 | tf_op jit(solution)/shard_map/while/body/eval_jaxpr/reduce_sum | solution.py:52
  103.8 0.7 gather_fusion
  104.4 0.1 fusion.17
  104.6 4.0 %fusion.18 = (f32[8,128]{1,0:T(8,128)S(1)}, f32[8,128]{1,0:T(8,128)S(1)}, f32[8,128]{1,0:T(8,128)S(1)}) fusion(f32[8,128]{1,0:T(8,128)S(1)} %get-tuple-element.133, f32[8,8,128]{2,1,0:T(8,128)S(1)} %bitcast.77, f32[8,128]{1,0:T(8,128)S(1)} %get-tuple-element.135, f32[8,8,128]{2,1,0:T(8,128)S(1)} %bitcast.78, f32[8,128]{1,0:T(8,128)S(1)} %get-tuple-element.137, ...), kind=kLoop, calls=%fused_computation.11.clone.1 | loop fusion | flops 17822720 | bytes 155648 | tf_op jit(solution)/shard_map/while/body/eval_jaxpr/reduce_sum | solution.py:52
  108.7 0.7 gather_fusion
  109.4 0.1 fusion.17
  109.5 4.0 %fusion.18 = (f32[8,128]{1,0:T(8,128)S(1)}, f32[8,128]{1,0:T(8,128)S(1)}, f32[8,128]{1,0:T(8,128)S(1)}) fusion(f32[8,128]{1,0:T(8,128)S(1)} %get-tuple-element.133, f32[8,8,128]{2,1,0:T(8,128)S(1)} %bitcast.77, f32[8,128]{1,0:T(8,128)S(1)} %get-tuple-element.135, f32[8,8,128]{2,1,0:T(8,128)S(1)} %bitcast.78, f32[8,128]{1,0:T(8,128)S(1)} %get-tuple-element.137, ...), kind=kLoop, calls=%fused_computation.11.clone.1 | loop fusion | flops 17822720 | bytes 155648 | tf_op jit(solution)/shard_map/while/body/eval_jaxpr/reduce_sum | solution.py:52
  113.7 0.7 gather_fusion
  114.3 0.1 fusion.17
  114.5 4.0 %fusion.18 = (f32[8,128]{1,0:T(8,128)S(1)}, f32[8,128]{1,0:T(8,128)S(1)}, f32[8,128]{1,0:T(8,128)S(1)}) fusion(f32[8,128]{1,0:T(8,128)S(1)} %get-tuple-element.133, f32[8,8,128]{2,1,0:T(8,128)S(1)} %bitcast.77, f32[8,128]{1,0:T(8,128)S(1)} %get-tuple-element.135, f32[8,8,128]{2,1,0:T(8,128)S(1)} %bitcast.78, f32[8,128]{1,0:T(8,128)S(1)} %get-tuple-element.137, ...), kind=kLoop, calls=%fused_computation.11.clone.1 | loop fusion | flops 17822720 | bytes 155648 | tf_op jit(solution)/shard_map/while/body/eval_jaxpr/reduce_sum | solution.py:52
  118.6 0.7 gather_fusion
  119.3 0.1 fusion.17
  119.4 4.0 %fusion.18 = (f32[8,128]{1,0:T(8,128)S(1)}, f32[8,128]{1,0:T(8,128)S(1)}, f32[8,128]{1,0:T(8,128)S(1)}) fusion(f32[8,128]{1,0:T(8,128)S(1)} %get-tuple-element.133, f32[8,8,128]{2,1,0:T(8,128)S(1)} %bitcast.77, f32[8,128]{1,0:T(8,128)S(1)} %get-tuple-element.135, f32[8,8,128]{2,1,0:T(8,128)S(1)} %bitcast.78, f32[8,128]{1,0:T(8,128)S(1)} %get-tuple-element.137, ...), kind=kLoop, calls=%fused_computation.11.clone.1 | loop fusion | flops 17822720 | bytes 155648 | tf_op jit(solution)/shard_map/while/body/eval_jaxpr/reduce_sum | solution.py:52
  123.6 0.7 gather_fusion
  124.3 0.1 fusion.17
  124.4 4.0 %fusion.18 = (f32[8,128]{1,0:T(8,128)S(1)}, f32[8,128]{1,0:T(8,128)S(1)}, f32[8,128]{1,0:T(8,128)S(1)}) fusion(f32[8,128]{1,0:T(8,128)S(1)} %get-tuple-element.133, f32[8,8,128]{2,1,0:T(8,128)S(1)} %bitcast.77, f32[8,128]{1,0:T(8,128)S(1)} %get-tuple-element.135, f32[8,8,128]{2,1,0:T(8,128)S(1)} %bitcast.78, f32[8,128]{1,0:T(8,128)S(1)} %get-tuple-element.137, ...), kind=kLoop, calls=%fused_computation.11.clone.1 | loop fusion | flops 17822720 | bytes 155648 | tf_op jit(solution)/shard_map/while/body/eval_jaxpr/reduce_sum | solution.py:52
  128.6 0.7 gather_fusion
  129.2 0.1 fusion.17
  129.4 4.0 %fusion.18 = (f32[8,128]{1,0:T(8,128)S(1)}, f32[8,128]{1,0:T(8,128)S(1)}, f32[8,128]{1,0:T(8,128)S(1)}) fusion(f32[8,128]{1,0:T(8,128)S(1)} %get-tuple-element.133, f32[8,8,128]{2,1,0:T(8,128)S(1)} %bitcast.77, f32[8,128]{1,0:T(8,128)S(1)} %get-tuple-element.135, f32[8,8,128]{2,1,0:T(8,128)S(1)} %bitcast.78, f32[8,128]{1,0:T(8,128)S(1)} %get-tuple-element.137, ...), kind=kLoop, calls=%fused_computation.11.clone.1 | loop fusion | flops 17822720 | bytes 155648 | tf_op jit(solution)/shard_map/while/body/eval_jaxpr/reduce_sum | solution.py:52
  133.5 0.7 gather_fusion
  134.3 4.0 %fusion.18 = (f32[8,128]{1,0:T(8,128)S(1)}, f32[8,128]{1,0:T(8,128)S(1)}, f32[8,128]{1,0:T(8,128)S(1)}) fusion(f32[8,128]{1,0:T(8,128)S(1)} %get-tuple-element.133, f32[8,8,128]{2,1,0:T(8,128)S(1)} %bitcast.77, f32[8,128]{1,0:T(8,128)S(1)} %get-tuple-element.135, f32[8,8,128]{2,1,0:T(8,128)S(1)} %bitcast.78, f32[8,128]{1,0:T(8,128)S(1)} %get-tuple-element.137, ...), kind=kLoop, calls=%fused_computation.11.clone.1 | loop fusion | flops 17822720 | bytes 155648 | tf_op jit(solution)/shard_map/while/body/eval_jaxpr/reduce_sum | solution.py:52
  138.5 0.7 gather_fusion
  139.3 4.0 %fusion.18 = (f32[8,128]{1,0:T(8,128)S(1)}, f32[8,128]{1,0:T(8,128)S(1)}, f32[8,128]{1,0:T(8,128)S(1)}) fusion(f32[8,128]{1,0:T(8,128)S(1)} %get-tuple-element.133, f32[8,8,128]{2,1,0:T(8,128)S(1)} %bitcast.77, f32[8,128]{1,0:T(8,128)S(1)} %get-tuple-element.135, f32[8,8,128]{2,1,0:T(8,128)S(1)} %bitcast.78, f32[8,128]{1,0:T(8,128)S(1)} %get-tuple-element.137, ...), kind=kLoop, calls=%fused_computation.11.clone.1 | loop fusion | flops 17822720 | bytes 155648 | tf_op jit(solution)/shard_map/while/body/eval_jaxpr/reduce_sum | solution.py:52
  143.3 0.8 copy.33
  (125 shorter events, 2.7 us)
Async XLA Ops:
  2.6 24.0 %all-to-all-start.1 = ((s32[1,64,2]{2,0,1:T(1,128)}), s32[1,64,2]{2,0,1:T(1,128)S(1)}, u32[]{:S(2)}, u32[]{:S(2)}) async-start(s32[1,64,2]{2,0,1:T(1,128)} %bitcast.16), calls=%async_computation.1 | async-start | bytes 65536 | tf_op jit(solution)/shard_map/all_to_all | solution.py:64
  26.7 17.9 %all-to-all-start = ((f32[4,64,256]{2,0,1:T(4,128)}), f32[4,64,256]{2,0,1:T(4,128)S(1)}, u32[]{:S(2)}, u32[]{:S(2)}) async-start(f32[4,64,256]{2,0,1:T(4,128)} %bitcast.15), calls=%async_computation | async-start | bytes 524288 | tf_op jit(solution)/shard_map/all_to_all | solution.py:17
  44.6 13.5 %copy-start = (s32[128,8]{0,1:T(8,128)S(1)}, s32[128,8]{0,1:T(8,128)}, u32[]{:S(2)}) copy-start(s32[128,8]{0,1:T(8,128)} %param.9) | copy-start | bytes 12292
  44.8 17.7 %collective-permute-start = (f32[128,4,128]{2,0,1:T(8,128)S(1)}, f32[128,4,128]{2,0,1:T(8,128)S(1)}, u32[]{:S(2)}, u32[]{:S(2)}) collective-permute-start(f32[128,4,128]{2,0,1:T(8,128)S(1)} %get-tuple-element.85), channel_id=1, source_target_pairs={{0,64},{64,128},{128,192},{192,256},{256,320},{320,384},{384,448},... | collective-permute-start | bytes 786440 | tf_op jit(solution)/shard_map/ppermute | solution.py:31
  46.7 16.7 %collective-permute-start.1 = (f32[128,4,128]{2,0,1:T(8,128)S(1)}, f32[128,4,128]{2,0,1:T(8,128)S(1)}, u32[]{:S(2)}, u32[]{:S(2)}) collective-permute-start(f32[128,4,128]{2,0,1:T(8,128)S(1)} %get-tuple-element.85), channel_id=1, source_target_pairs={{64,0},{128,64},{192,128},{256,192},{320,256},{384,320},{448,384},... | collective-permute-start | bytes 786440 | tf_op jit(solution)/shard_map/ppermute | solution.py:32
where the time goes:
time: 144 us
  other arithmetic  68.5 us (48%)
  starting transfers between devices  32.4 us (22%)
  waiting for transfers between devices  25.1 us (17%)
  local copies, waits for them, and re-layouts  16.8 us (12%)
    reduce_sum x16, other arithmetic, one_group(): pull_x = jnp.sum(weight * delta_x, axis=(1, 3))  64 us
    all_to_all x1, starting transfers between devices, on_device(): lax.all_to_all(counts, 'col', split_axis=1, concat_axis=1, tiled=True)  14.5 us
    all_to_all x1, waiting for transfers between devices, sent_together(): lax.all_to_all(both, axis, split_axis=split_dim, concat_axis=concat_dim,...  12.3 us
    ppermute x1, starting transfers between devices, padded_2(): after = lax.ppermute(leading, axis, down)  11.3 us
    gather x16, local copies, waits for them, and re-layouts, one_group(): source = full_table[index]  10.5 us
    all_to_all x1, waiting for transfers between devices, on_device(): lax.all_to_all(counts, 'col', split_axis=1, concat_axis=1, tiled=True)  7.7 us
    all_to_all x1, starting transfers between devices, sent_together(): lax.all_to_all(both, axis, split_axis=split_dim, concat_axis=concat_dim,...  4.71 us
    ppermute x1, waiting for transfers between devices, padded_2(): before = lax.ppermute(last, axis, up)  4.18 us
  transfers between devices with their start and end apart: 4, of which 4 were waited for; matrix products, arithmetic and copies ran while one was open for 2% of the time, Pallas kernels for 0%

commit v1 on v0

v1 whole, which is shorter than its diff:
```python
import jax
import jax.numpy as jnp
from jax import lax
from jax.experimental import pallas as pl
from jax.experimental.pallas import tpu as pltpu
from jax.sharding import PartitionSpec as P

softening = 2.5e-07
LEAVES = 128
SLOTS = 128
NEAR = 32
DEAD = -1.0
MIB = 1024 * 1024


def pack_kernel(positions, masses, counts, out):
    lane = lax.broadcasted_iota(jnp.int32, (1, SLOTS), 1)

    def group(first, _):
        for part in range(8):
            leaf = first * 8 + part
            at = pl.multiple_of(leaf * SLOTS, SLOTS)
            out[leaf, 0:3, :] = positions[:, pl.ds(at, SLOTS)]
            out[leaf, 3:4, :] = jnp.where(lane < counts[0, leaf], masses[:, pl.ds(at, SLOTS)], DEAD)
        return 0

    lax.fori_loop(0, LEAVES // 8, group, 0)


def plan_kernel(sources, slot_of, picked):
    low = lax.broadcasted_iota(jnp.int32, (2 * LEAVES, SLOTS), 0) + LEAVES
    named = jnp.zeros((2 * LEAVES, SLOTS), jnp.bool_)
    for k in range(8):
        named = named | (low == sources[k : k + 1, :])
    flags = named.astype(jnp.float32).astype(jnp.bfloat16)
    ones = jnp.ones((8, SLOTS), jnp.bfloat16)
    lanes = (((1,), (1,)), ((), ()))
    uses = lax.dot_general(ones, flags, lanes, preferred_element_type=jnp.float32)
    present = uses > 0.5
    row = lax.broadcasted_iota(jnp.int32, (2 * LEAVES, 2 * LEAVES), 0)
    col = lax.broadcasted_iota(jnp.int32, (2 * LEAVES, 2 * LEAVES), 1)
    before = (row < col).astype(jnp.float32).astype(jnp.bfloat16)
    ahead = present.astype(jnp.float32).astype(jnp.bfloat16)
    rank = lax.dot_general(ahead, before, (((1,), (0,)), ((), ())), preferred_element_type=jnp.float32)
    rank = rank.astype(jnp.int32)
    slot_of[...] = jnp.minimum(rank, 2 * NEAR - 1)
    slot = lax.broadcasted_iota(jnp.int32, (SLOTS, 2 * LEAVES), 0)
    chosen = (slot == jnp.where(present, rank, -1)[0:1, :]).astype(jnp.float32).astype(jnp.bfloat16)
    leaf = lax.broadcasted_iota(jnp.int32, (8, 2 * LEAVES), 1) & (LEAVES - 1)
    leaf = leaf.astype(jnp.float32).astype(jnp.bfloat16)
    picked[...] = lax.dot_general(leaf, chosen, lanes, preferred_element_type=jnp.float32).astype(jnp.int32)


def pair_forces(source_table, target_table, ids, spread, sums, stage, chunks_vmem, chunks_smem, sem, leaves):
    null_chunk = leaves * 8
    ones = jnp.ones((8, SLOTS), jnp.bfloat16)
    live = (source_table[:, 3, :] >= 0.0).astype(jnp.float32).astype(jnp.bfloat16)
    if leaves < SLOTS:
        live = jnp.concatenate([live, jnp.zeros((SLOTS - leaves, SLOTS), jnp.bfloat16)], axis=0)
    count = lax.dot_general(ones, live, (((1,), (1,)), ((), ())), preferred_element_type=jnp.float32)
    size = (count.astype(jnp.int32) + 15) >> 4
    mine = ids >= 0
    leaf = jnp.where(mine, ids, 0)
    size = jnp.where(mine, jnp.take_along_axis(size, leaf, axis=1), 0)
    sub = lax.broadcasted_iota(jnp.int32, (8, SLOTS), 0)
    starts, shifts, total = [], [], jnp.zeros((8, SLOTS), jnp.int32)
    for k in range(8):
        starts.append(total)
        shifts.append(jnp.broadcast_to(leaf[k : k + 1, :], (8, SLOTS)) * 8 - total)
        total = total + jnp.broadcast_to(size[k : k + 1, :], (8, SLOTS))
    for part in range(8):
        at = sub + 8 * part
        chunk = at + shifts[0]
        for k in range(1, 8):
            chunk = jnp.where(at >= starts[k], at + shifts[k], chunk)
        chunks_vmem[8 * part : 8 * part + 8, :] = jnp.where(at < total, chunk, null_chunk)
    chunks_vmem[64:72, :] = total
    to_scalars = pltpu.make_async_copy(chunks_vmem, chunks_smem, sem)
    to_scalars.start()

    unit = 4

    def spread_leaf(first, _):
        rows = []
        for u in range(unit):
            for c in range(4):
                row = source_table[first * unit + u, c : c + 1, :]
                rows.append(jnp.broadcast_to(jnp.maximum(row, 0.0) if c == 3 else row, (8, SLOTS)))
        for block in range(16):
            index = sub + 8 * block
            for u in range(unit):
                for c in range(4):
                    spread[(first * unit + u) * 16 + block, 8 * c : 8 * c + 8, :] = jnp.take_along_axis(
                        rows[u * 4 + c], index, axis=1
                    )
        return 0

    lax.fori_loop(0, leaves // unit, spread_leaf, 0)
    for block in range(2):
        spread[leaves * 16 + block] = jnp.zeros((32, SLOTS), jnp.float32)
    stage[:, 0:32, :] = jnp.zeros((8, 32, SLOTS), jnp.float32)
    stage[:, 32:40, :] = jnp.ones((8, 8, SLOTS), jnp.float32)

    def clear(i, _):
        for part in range(8):
            sums[i * 8 + part] = jnp.zeros((24, SLOTS), jnp.float32)
        return 0

    lax.fori_loop(0, LEAVES // 8, clear, 0)
    to_scalars.wait()

    def staged(u):
        return [stage[u, 8 * c : 8 * c + 8, :] for c in range(4)]

    def add_staged(old, r, pulls):
        weight = (old[3] * r) * (r * r)
        parts = [weight * old[c] for c in range(3)]
        return parts if pulls is None else [a + b for a, b in zip(pulls, parts)]

    def fill_stage(u, block, centre):
        dx, dy, dz = (spread[block, 8 * c : 8 * c + 8, :] - centre[c] for c in range(3))
        stage[u, 0:8, :] = dx
        stage[u, 8:16, :] = dy
        stage[u, 16:24, :] = dz
        stage[u, 24:32, :] = spread[block, 24:32, :]
        stage[u, 32:40, :] = (dx * dx + softening) + (dy * dy + dz * dz)

    def add_to_sums(target, pulls):
        for c in range(3):
            sums[target, 8 * c : 8 * c + 8, :] += pulls[c]

    def chunks_at(target, at):
        return tuple(chunks_smem[at + i, target] * 2 for i in range(4))

    def body(state):
        target, at, old_target, chunks = state
        centre = [jnp.broadcast_to(target_table[target, c : c + 1, :], (8, SLOTS)) for c in range(3)]
        roots = [lax.rsqrt(stage[u, 32:40, :]) for u in range(8)]
        pulls = None
        for u in range(8):
            old = staged(u)
            fill_stage(u, chunks[u // 2] + u % 2, centre)
            pulls = add_staged(old, roots[u], pulls)
        add_to_sums(old_target, pulls)
        done = at + 4 >= chunks_smem[64, target]
        after = jnp.where(done, target + 1, target)
        at = jnp.where(done, 0, at + 4)
        return after, at, target, chunks_at(jnp.minimum(after, LEAVES - 1), at)

    zero = jnp.int32(0)
    state = lax.while_loop(lambda s: s[0] < LEAVES, body, (zero, zero, zero, chunks_at(zero, zero)))
    pulls = None
    for u in range(8):
        pulls = add_staged(staged(u), lax.rsqrt(stage[u, 32:40, :]), pulls)
    add_to_sums(state[2], pulls)


def own_kernel(table, sources, out, spread, sums, stage, chunks_vmem, chunks_smem, sem):
    ids = sources[...]
    ids = jnp.where(ids < LEAVES, ids, -1)
    pair_forces(table, table, ids, spread, sums, stage, chunks_vmem, chunks_smem, sem, LEAVES)

    def finish(i, _):
        for part in range(8):
            t = i * 8 + part
            for c in range(3):
                out[t, c : c + 1, :] = jnp.sum(sums[t, 8 * c : 8 * c + 8, :], axis=0, keepdims=True)
        return 0

    lax.fori_loop(0, LEAVES // 8, finish, 0)


def near_kernel(before, after, table, own_pull, sources, slot_of, picked, out, leaves, spread, sums, stage, chunks_vmem, chunks_smem, sem):
    def gather(i, _):
        for part in range(8):
            s = i * 8 + part
            leaves[s] = before[picked[0, s]]
            leaves[NEAR + s] = after[picked[0, NEAR + s]]
        return 0

    lax.fori_loop(0, NEAR // 8, gather, 0)
    ids = sources[...]
    within = ids & (LEAVES - 1)
    below = jnp.take_along_axis(slot_of[:, :LEAVES], within, axis=1)
    above = jnp.take_along_axis(slot_of[:, LEAVES:], within, axis=1)
    ids = jnp.where(ids < LEAVES, -1, jnp.where(ids < 2 * LEAVES, below, above))
    pair_forces(leaves, table, ids, spread, sums, stage, chunks_vmem, chunks_smem, sem, 2 * NEAR)

    def finish(i, _):
        for part in range(8):
            t = i * 8 + part
            at = pl.multiple_of(t * SLOTS, SLOTS)
            living = table[t, 3:4, :] >= 0.0
            for c in range(3):
                pull = jnp.sum(sums[t, 8 * c : 8 * c + 8, :], axis=0, keepdims=True) + own_pull[t, c : c + 1, :]
                out[c : c + 1, pl.ds(at, SLOTS)] = jnp.where(living, pull, 0.0)
        return 0

    lax.fori_loop(0, LEAVES // 8, finish, 0)


def f32(*shape):
    return jax.ShapeDtypeStruct(shape, jnp.float32)


def i32(*shape):
    return jax.ShapeDtypeStruct(shape, jnp.int32)


vmem = pl.BlockSpec(memory_space=pltpu.VMEM)
smem = pl.BlockSpec(memory_space=pltpu.SMEM)


def pair_scratch(leaves):
    return [
        pltpu.VMEM((leaves * 16 + 2, 32, SLOTS), jnp.float32),
        pltpu.VMEM((LEAVES, 24, SLOTS), jnp.float32),
        pltpu.VMEM((8, 40, SLOTS), jnp.float32),
        pltpu.VMEM((72, SLOTS), jnp.int32),
        pltpu.SMEM((72, SLOTS), jnp.int32),
        pltpu.SemaphoreType.DMA,
    ]


def cost(us):
    return pl.CostEstimate(flops=int(us * 8_000_000), bytes_accessed=0, transcendentals=0)


def pack(positions, masses, counts):
    return pl.pallas_call(
        pack_kernel,
        out_shape=f32(LEAVES, 4, SLOTS),
        in_specs=[vmem, vmem, smem],
        out_specs=vmem,
        name="pack",
    )(positions, masses, counts)


def plan(sources):
    return pl.pallas_call(
        plan_kernel,
        out_shape=(i32(8, 2 * LEAVES), i32(8, SLOTS)),
        in_specs=[vmem],
        out_specs=(vmem, vmem),
        cost_estimate=cost(1),
        name="plan",
    )(sources)


def own_forces(table, sources):
    return pl.pallas_call(
        own_kernel,
        out_shape=f32(LEAVES, 4, SLOTS),
        in_specs=[vmem, vmem],
        out_specs=vmem,
        scratch_shapes=pair_scratch(LEAVES),
        compiler_params=pltpu.CompilerParams(vmem_limit_bytes=42 * MIB),
        cost_estimate=cost(20),
        name="own_forces",
    )(table, sources)


def near_forces(before, after, table, own_pull, sources, slot_of, picked):
    return pl.pallas_call(
        near_kernel,
        out_shape=f32(3, LEAVES * SLOTS),
        in_specs=[vmem, vmem, vmem, vmem, vmem, vmem, smem],
        out_specs=vmem,
        scratch_shapes=[pltpu.VMEM((2 * NEAR, 4, SLOTS), jnp.float32)] + pair_scratch(2 * NEAR),
        compiler_params=pltpu.CompilerParams(vmem_limit_bytes=30 * MIB),
        cost_estimate=cost(12),
        name="near_forces",
    )(before, after, table, own_pull, sources, slot_of, picked)


def on_device(positions, masses, counts, sources):
    sources = sources.T
    sent = pack(positions, masses, counts)
    slot_of, picked = plan(sources)
    table = lax.all_to_all(sent, "col", split_axis=0, concat_axis=0, tiled=True)
    size = lax.axis_size("row")
    up = [(i, (i + 1) % size) for i in range(size)]
    down = [(j, i) for i, j in up]
    before = lax.ppermute(table, "row", up)
    after = lax.ppermute(table, "row", down)
    own_pull = own_forces(table, sources)
    return near_forces(before, after, table, own_pull, sources, slot_of, picked)


def solution(mesh):
    return jax.shard_map(
        on_device,
        mesh=mesh,
        in_specs=(
            P(None, ("row", "col")),
            P(None, ("row", "col")),
            P(None, ("row", "col")),
            P(("row", "col"), None),
        ),
        out_specs=P(None, ("row", "col")),
        check_vma=False,
    )
```

time: 144 us -> 109 us (0.76); the launches traced: 144 us -> 107 us
  other arithmetic: 68.5 us -> 0 us
  Pallas kernels: 0 us -> 66 us
  blocking collectives: 0 us -> 27.7 us
  waiting for transfers between devices: 25.1 us -> 0.01 us
  starting transfers between devices: 32.4 us -> 13.2 us
  local copies, waits for them, and re-layouts: 16.8 us -> 0.01 us
    pallas_call x0 -> x4, Pallas kernels: none -> 66 us  [the longest x1 38.5 us: own_forces(): pl.pallas_call(own_kernel, out_shape=f32(LEAVES, 4, SLOTS), in_specs=[vme...]
    reduce_sum x16 -> x0, other arithmetic: 64 us -> none  [one_group(): pull_x = jnp.sum(weight * delta_x, axis=(1, 3))]
    all_to_all x0 -> x1, blocking collectives: none -> 27.7 us  [on_device(): table = lax.all_to_all(sent, 'col', split_axis=0, concat_axis=0, tiled=True)]
    all_to_all x2 -> x0, waiting for transfers between devices: 20 us -> none  [the longest x1 12.3 us: sent_together(): lax.all_to_all(both, axis, split_axis=split_dim, concat_axis=concat_dim,...]
    all_to_all x2 -> x0, starting transfers between devices: 19.2 us -> none  [the longest x1 14.5 us: on_device(): lax.all_to_all(counts, 'col', split_axis=1, concat_axis=1, tiled=True)]
    gather x16 -> x0, local copies, waits for them, and re-layouts: 10.5 us -> none  [one_group(): source = full_table[index]]
    ppermute x2, waiting for transfers between devices: 5.08 us -> 0.01 us  [the longest x1 0.01 us: on_device(): before = lax.ppermute(table, 'row', up)]
    concatenate x2 -> x0, other arithmetic: 1.87 us -> none  [the longest x1 1.81 us: sent_together(): both = jnp.concatenate(arrays, axis=along)]
  transfers between devices with their start and end apart: 4 -> 2, of which waited for: 4 -> 0; matrix products, arithmetic and copies ran while one was open for 2% -> 0% of each run, Pallas kernels for 0% -> 38%
where the time goes in v1:
time: 109 us; the launch traced here: 107 us
  Pallas kernels  66 us (61%)
  blocking collectives  27.7 us (25%)
  starting transfers between devices  13.2 us (12%)
    pallas_call x1, Pallas kernels, own_forces(): pl.pallas_call(own_kernel, out_shape=f32(LEAVES, 4, SLOTS), in_specs=[vme...  38.5 us
    all_to_all x1, blocking collectives, on_device(): table = lax.all_to_all(sent, 'col', split_axis=0, concat_axis=0, tiled=True)  27.7 us
    pallas_call x1, Pallas kernels, near_forces(): pl.pallas_call(near_kernel, out_shape=f32(3, LEAVES * SLOTS), in_specs=[v...  23.7 us
    ppermute x1, starting transfers between devices, on_device(): after = lax.ppermute(table, 'row', down)  11.2 us
  transfers between devices with their start and end apart: 2, of which 0 were waited for; matrix products, arithmetic and copies ran while one was open for 0% of the time, Pallas kernels for 38%

profile of v1, /device:TPU:1, one launch (start us, length us, event | category | flops | bytes accessed | tf_op | source)
XLA Modules:
  0.0 107.0 jit_solution(3563513729488159012)
XLA Ops:
  0.0 2.0 %pack.1 = f32[128,4,128]{2,1,0:T(4,128)} custom-call(f32[3,16384]{1,0:T(4,128)} %positions.1, f32[1,16384]{1,0:T(1,128)} %masses.1, s32[1,128]{1,0:T(1,128)} %counts.1), custom_call_target="tpu_custom_call" | custom-call | tf_op jit(solution)/shard_map/pack/pallas_call | solution.py:230
  2.0 27.7 %all_to_all.5.table = f32[128,4,128]{2,1,0:T(4,128)S(1)} all-to-all(f32[128,4,128]{2,1,0:T(4,128)} %pack.1), channel_id=1, replica_groups=mesh['row'=12,'col'=64] {'col'}, dimensions={0} | all-to-all | bytes 524288 | tf_op jit(solution)/shard_map/all_to_all | solution.py:280
  29.7 11.2 %collective-permute-start.1 = (f32[128,4,128]{2,1,0:T(4,128)S(1)}, f32[128,4,128]{2,1,0:T(4,128)S(1)}, u32[]{:S(2)}, u32[]{:S(2)}) collective-permute-start(f32[128,4,128]{2,1,0:T(4,128)S(1)} %all_to_all.5.table), channel_id=1, source_target_pairs={{64,0},{128,64},{192,128},{256,192},{320,256},{384,320},{448,384},... | collective-permute-start | bytes 786440 | tf_op jit(solution)/shard_map/ppermute | solution.py:285
  41.0 1.9 %collective-permute-start = (f32[128,4,128]{2,1,0:T(4,128)S(1)}, f32[128,4,128]{2,1,0:T(4,128)S(1)}, u32[]{:S(2)}, u32[]{:S(2)}) collective-permute-start(f32[128,4,128]{2,1,0:T(4,128)S(1)} %all_to_all.5.table), channel_id=1, source_target_pairs={{0,64},{64,128},{128,192},{192,256},{256,320},{320,384},{384,448},... | collective-permute-start | bytes 786440 | tf_op jit(solution)/shard_map/ppermute | solution.py:284
  42.9 0.0 copy-start.1
  42.9 1.9 %plan.1 = (s32[8,256]{1,0:T(8,128)}, s32[8,128]{1,0:T(8,128)}) custom-call(s32[8,128]{1,0:T(8,128)} %bitcast.1), custom_call_target="tpu_custom_call" | custom-call | flops 8000000 | tf_op jit(solution)/shard_map/plan/pallas_call | solution.py:240
  44.8 0.0 copy-done.1
  44.8 0.0 copy-start
  44.8 0.0 copy-start.2
  44.8 38.5 %own_forces.1.own_pull = f32[128,4,128]{2,1,0:T(4,128)S(1)} custom-call(f32[128,4,128]{2,1,0:T(4,128)S(1)} %all_to_all.5.table, s32[8,128]{1,0:T(8,128)S(1)} %bitcast.2), custom_call_target="tpu_custom_call" | custom-call | flops 160000000 | tf_op jit(solution)/shard_map/own_forces/pallas_call | solution.py:251
  83.3 0.0 collective-permute-done.1.after
  83.3 0.0 collective-permute-done.before
  83.3 0.0 copy-done
  83.3 0.0 copy-done.2
  83.3 23.7 %near_forces.1 = f32[3,16384]{1,0:T(4,128)} custom-call(f32[128,4,128]{2,1,0:T(4,128)S(1)} %collective-permute-done.before, f32[128,4,128]{2,1,0:T(4,128)S(1)} %collective-permute-done.1.after, f32[128,4,128]{2,1,0:T(4,128)S(1)} %all_to_all.5.table, f32[128,4,128]{2,1,0:T(4,128)S(1)} %own_forces.1.own_pull, s32[8,128]{1,0:T(8,128)S(1)} %bitcast.3, ...), custom_call_target="tpu_custom_call" | custom-call | flops 96000000 | tf_op jit(solution)/shard_map/near_forces/pallas_call | solution.py:264
Async XLA Ops:
  29.7 53.5 %collective-permute-start.1 = (f32[128,4,128]{2,1,0:T(4,128)S(1)}, f32[128,4,128]{2,1,0:T(4,128)S(1)}, u32[]{:S(2)}, u32[]{:S(2)}) collective-permute-start(f32[128,4,128]{2,1,0:T(4,128)S(1)} %all_to_all.5.table), channel_id=1, source_target_pairs={{64,0},{128,64},{192,128},{256,192},{320,256},{384,320},{448,384},... | collective-permute-start | bytes 786440 | tf_op jit(solution)/shard_map/ppermute | solution.py:285
  41.0 42.3 %collective-permute-start = (f32[128,4,128]{2,1,0:T(4,128)S(1)}, f32[128,4,128]{2,1,0:T(4,128)S(1)}, u32[]{:S(2)}, u32[]{:S(2)}) collective-permute-start(f32[128,4,128]{2,1,0:T(4,128)S(1)} %all_to_all.5.table), channel_id=1, source_target_pairs={{0,64},{64,128},{128,192},{192,256},{256,320},{320,384},{384,448},... | collective-permute-start | bytes 786440 | tf_op jit(solution)/shard_map/ppermute | solution.py:284
  42.9 1.9 %copy-start.1 = (s32[128,8]{0,1:T(8,128)S(1)}, s32[128,8]{0,1:T(8,128)}, u32[]{:S(2)}) copy-start(s32[128,8]{0,1:T(8,128)} %param.7) | copy-start | bytes 12292
  44.8 38.5 %copy-start = (s32[8,256]{1,0:T(8,128)S(1)}, s32[8,256]{1,0:T(8,128)}, u32[]{:S(2)}) copy-start(s32[8,256]{1,0:T(8,128)} %get-tuple-element.7.slot_of) | copy-start | bytes 24580
  44.8 38.5 %copy-start.2 = (s32[8,128]{1,0:T(8,128)S(1)}, s32[8,128]{1,0:T(8,128)}, u32[]{:S(2)}) copy-start(s32[8,128]{1,0:T(8,128)} %get-tuple-element.8.picked) | copy-start | bytes 12292

commit v2 on v1

--- a/solution.py
+++ b/solution.py
@@ -6,6 +6,8 @@
 from jax.sharding import PartitionSpec as P
 
 softening = 2.5e-07
+unit = 16
+blocks = 8
 LEAVES = 128
 SLOTS = 128
 NEAR = 32
@@ -27,7 +29,7 @@
     lax.fori_loop(0, LEAVES // 8, group, 0)
 
 
-def plan_kernel(sources, slot_of, picked):
+def number_neighbours(sources, slot_of, picked):
     low = lax.broadcasted_iota(jnp.int32, (2 * LEAVES, SLOTS), 0) + LEAVES
     named = jnp.zeros((2 * LEAVES, SLOTS), jnp.bool_)
     for k in range(8):
@@ -51,7 +53,7 @@
     picked[...] = lax.dot_general(leaf, chosen, lanes, preferred_element_type=jnp.float32).astype(jnp.int32)
 
 
-def pair_forces(source_table, target_table, ids, spread, sums, stage, chunks_vmem, chunks_smem, sem, leaves):
+def pair_forces(source_table, target_table, ids, spread, sums, chunks_vmem, chunks_smem, sem, leaves):
     null_chunk = leaves * 8
     ones = jnp.ones((8, SLOTS), jnp.bfloat16)
     live = (source_table[:, 3, :] >= 0.0).astype(jnp.float32).astype(jnp.bfloat16)
@@ -75,31 +77,37 @@
             chunk = jnp.where(at >= starts[k], at + shifts[k], chunk)
         chunks_vmem[8 * part : 8 * part + 8, :] = jnp.where(at < total, chunk, null_chunk)
     chunks_vmem[64:72, :] = total
+    chunks_vmem[72:80, :] = jnp.full((8, SLOTS), null_chunk, jnp.int32)
     to_scalars = pltpu.make_async_copy(chunks_vmem, chunks_smem, sem)
     to_scalars.start()
 
-    unit = 4
+    limb = lax.broadcasted_iota(jnp.int32, (16, 4 * SLOTS), 0)
+    column = lax.broadcasted_iota(jnp.int32, (16, 4 * SLOTS), 1)
+    gather = ((limb < 12) & ((limb & 3) == column // SLOTS)).astype(jnp.float32).astype(jnp.bfloat16)
+
+    def limbs_of(tile):
+        high = tile.astype(jnp.bfloat16).astype(jnp.float32)
+        rest = tile - high
+        middle = rest.astype(jnp.bfloat16).astype(jnp.float32)
+        low = rest - middle
+        return jnp.concatenate([high, middle, low, jnp.zeros((4, SLOTS), jnp.float32)], axis=0)
+
+    value = lax.broadcasted_iota(jnp.int32, (4, SLOTS), 0)
 
     def spread_leaf(first, _):
-        rows = []
+        lhs = []
         for u in range(unit):
-            for c in range(4):
-                row = source_table[first * unit + u, c : c + 1, :]
-                rows.append(jnp.broadcast_to(jnp.maximum(row, 0.0) if c == 3 else row, (8, SLOTS)))
-        for block in range(16):
-            index = sub + 8 * block
-            for u in range(unit):
-                for c in range(4):
-                    spread[(first * unit + u) * 16 + block, 8 * c : 8 * c + 8, :] = jnp.take_along_axis(
-                        rows[u * 4 + c], index, axis=1
-                    )
+            tile = source_table[first * unit + u]
+            tile = jnp.where(value == 3, jnp.maximum(tile, 0.0), tile)
+            lhs.append(jnp.transpose(limbs_of(tile)).astype(jnp.bfloat16))
+        at = pl.multiple_of(first * (unit * SLOTS), unit * SLOTS)
+        spread[pl.ds(at, unit * SLOTS), :] = jnp.dot(
+            jnp.concatenate(lhs, axis=0), gather, preferred_element_type=jnp.float32
+        )
         return 0
 
     lax.fori_loop(0, leaves // unit, spread_leaf, 0)
-    for block in range(2):
-        spread[leaves * 16 + block] = jnp.zeros((32, SLOTS), jnp.float32)
-    stage[:, 0:32, :] = jnp.zeros((8, 32, SLOTS), jnp.float32)
-    stage[:, 32:40, :] = jnp.ones((8, 8, SLOTS), jnp.float32)
+    spread[leaves * SLOTS : leaves * SLOTS + 16, :] = jnp.zeros((16, 4 * SLOTS), jnp.float32)
 
     def clear(i, _):
         for part in range(8):
@@ -109,23 +117,18 @@
     lax.fori_loop(0, LEAVES // 8, clear, 0)
     to_scalars.wait()
 
-    def staged(u):
-        return [stage[u, 8 * c : 8 * c + 8, :] for c in range(4)]
-
-    def add_staged(old, r, pulls):
-        weight = (old[3] * r) * (r * r)
-        parts = [weight * old[c] for c in range(3)]
-        return parts if pulls is None else [a + b for a, b in zip(pulls, parts)]
-
-    def fill_stage(u, block, centre):
-        dx, dy, dz = (spread[block, 8 * c : 8 * c + 8, :] - centre[c] for c in range(3))
-        stage[u, 0:8, :] = dx
-        stage[u, 8:16, :] = dy
-        stage[u, 16:24, :] = dz
-        stage[u, 24:32, :] = spread[block, 24:32, :]
-        stage[u, 32:40, :] = (dx * dx + softening) + (dy * dy + dz * dz)
-
-    def add_to_sums(target, pulls):
+    def pull_on(target, chunks):
+        centre = [jnp.broadcast_to(target_table[target, c : c + 1, :], (8, SLOTS)) for c in range(3)]
+        pulls = None
+        for u in range(8):
+            block = chunks[u // 2] + u % 2
+            rows = pl.ds(pl.multiple_of(block * 8, 8), 8)
+            delta = [spread[rows, SLOTS * c : SLOTS * c + SLOTS] - centre[c] for c in range(3)]
+            squares = [d * d for d in delta]
+            r = lax.rsqrt((squares[0] + softening) + (squares[1] + squares[2]))
+            weight = (spread[rows, 3 * SLOTS : 4 * SLOTS] * r) * (r * r)
+            parts = [weight * d for d in delta]
+            pulls = parts if pulls is None else [a + b for a, b in zip(pulls, parts)]
         for c in range(3):
             sums[target, 8 * c : 8 * c + 8, :] += pulls[c]
 
@@ -133,32 +136,26 @@
         return tuple(chunks_smem[at + i, target] * 2 for i in range(4))
 
     def body(state):
-        target, at, old_target, chunks = state
-        centre = [jnp.broadcast_to(target_table[target, c : c + 1, :], (8, SLOTS)) for c in range(3)]
-        roots = [lax.rsqrt(stage[u, 32:40, :]) for u in range(8)]
-        pulls = None
-        for u in range(8):
-            old = staged(u)
-            fill_stage(u, chunks[u // 2] + u % 2, centre)
-            pulls = add_staged(old, roots[u], pulls)
-        add_to_sums(old_target, pulls)
-        done = at + 4 >= chunks_smem[64, target]
-        after = jnp.where(done, target + 1, target)
-        at = jnp.where(done, 0, at + 4)
-        return after, at, target, chunks_at(jnp.minimum(after, LEAVES - 1), at)
+        target, at, chunks = state
+        for _ in range(blocks):
+            pull_on(target, chunks)
+            at = at + 4
+            done = at >= chunks_smem[64, target]
+            over = done & (target == LEAVES - 1)
+            target = jnp.where(done & ~over, target + 1, target)
+            at = jnp.where(over, 72, jnp.where(done, 0, at))
+            chunks = chunks_at(target, at)
+        return target, at, chunks
 
     zero = jnp.int32(0)
-    state = lax.while_loop(lambda s: s[0] < LEAVES, body, (zero, zero, zero, chunks_at(zero, zero)))
-    pulls = None
-    for u in range(8):
-        pulls = add_staged(staged(u), lax.rsqrt(stage[u, 32:40, :]), pulls)
-    add_to_sums(state[2], pulls)
-
-
-def own_kernel(table, sources, out, spread, sums, stage, chunks_vmem, chunks_smem, sem):
+    lax.while_loop(lambda s: s[1] < 72, body, (zero, zero, chunks_at(zero, zero)))
+
+
+def own_kernel(table, sources, out, slot_of, picked, spread, sums, chunks_vmem, chunks_smem, sem):
     ids = sources[...]
     ids = jnp.where(ids < LEAVES, ids, -1)
-    pair_forces(table, table, ids, spread, sums, stage, chunks_vmem, chunks_smem, sem, LEAVES)
+    number_neighbours(sources, slot_of, picked)
+    pair_forces(table, table, ids, spread, sums, chunks_vmem, chunks_smem, sem, LEAVES)
 
     def finish(i, _):
         for part in range(8):
@@ -170,7 +167,7 @@
     lax.fori_loop(0, LEAVES // 8, finish, 0)
 
 
-def near_kernel(before, after, table, own_pull, sources, slot_of, picked, out, leaves, spread, sums, stage, chunks_vmem, chunks_smem, sem):
+def near_kernel(before, after, table, own_pull, sources, slot_of, picked, out, leaves, spread, sums, chunks_vmem, chunks_smem, sem):
     def gather(i, _):
         for part in range(8):
             s = i * 8 + part
@@ -184,7 +181,7 @@
     below = jnp.take_along_axis(slot_of[:, :LEAVES], within, axis=1)
     above = jnp.take_along_axis(slot_of[:, LEAVES:], within, axis=1)
     ids = jnp.where(ids < LEAVES, -1, jnp.where(ids < 2 * LEAVES, below, above))
-    pair_forces(leaves, table, ids, spread, sums, stage, chunks_vmem, chunks_smem, sem, 2 * NEAR)
+    pair_forces(leaves, table, ids, spread, sums, chunks_vmem, chunks_smem, sem, 2 * NEAR)
 
     def finish(i, _):
         for part in range(8):
@@ -213,11 +210,10 @@
 
 def pair_scratch(leaves):
     return [
-        pltpu.VMEM((leaves * 16 + 2, 32, SLOTS), jnp.float32),
+        pltpu.VMEM((leaves * SLOTS + 16, 4 * SLOTS), jnp.float32),
         pltpu.VMEM((LEAVES, 24, SLOTS), jnp.float32),
-        pltpu.VMEM((8, 40, SLOTS), jnp.float32),
-        pltpu.VMEM((72, SLOTS), jnp.int32),
-        pltpu.SMEM((72, SLOTS), jnp.int32),
+        pltpu.VMEM((80, SLOTS), jnp.int32),
+        pltpu.SMEM((80, SLOTS), jnp.int32),
         pltpu.SemaphoreType.DMA,
     ]
 
@@ -236,23 +232,12 @@
     )(positions, masses, counts)
 
 
-def plan(sources):
-    return pl.pallas_call(
-        plan_kernel,
-        out_shape=(i32(8, 2 * LEAVES), i32(8, SLOTS)),
-        in_specs=[vmem],
-        out_specs=(vmem, vmem),
-        cost_estimate=cost(1),
-        name="plan",
-    )(sources)
-
-
 def own_forces(table, sources):
     return pl.pallas_call(
         own_kernel,
-        out_shape=f32(LEAVES, 4, SLOTS),
+        out_shape=(f32(LEAVES, 4, SLOTS), i32(8, 2 * LEAVES), i32(8, SLOTS)),
         in_specs=[vmem, vmem],
-        out_specs=vmem,
+        out_specs=(vmem, vmem, vmem),
         scratch_shapes=pair_scratch(LEAVES),
         compiler_params=pltpu.CompilerParams(vmem_limit_bytes=42 * MIB),
         cost_estimate=cost(20),
@@ -276,14 +261,13 @@
 def on_device(positions, masses, counts, sources):
     sources = sources.T
     sent = pack(positions, masses, counts)
-    slot_of, picked = plan(sources)
     table = lax.all_to_all(sent, "col", split_axis=0, concat_axis=0, tiled=True)
     size = lax.axis_size("row")
     up = [(i, (i + 1) % size) for i in range(size)]
     down = [(j, i) for i, j in up]
     before = lax.ppermute(table, "row", up)
     after = lax.ppermute(table, "row", down)
-    own_pull = own_forces(table, sources)
+    own_pull, slot_of, picked = own_forces(table, sources)
     return near_forces(before, after, table, own_pull, sources, slot_of, picked)
 
 

time: 109 us -> 91.7 us (0.84); the launches traced: 107 us -> 91.2 us
  Pallas kernels: 66 us -> 50.1 us
    pallas_call x2 -> x1, Pallas kernels: 40.3 us -> 29.3 us  [own_forces(): pl.pallas_call(own_kernel, out_shape=(f32(LEAVES, 4, SLOTS), i32(8, 2 * L...]
    pallas_call x1, Pallas kernels: 23.7 us -> 18.9 us  [near_forces(): pl.pallas_call(near_kernel, out_shape=f32(3, LEAVES * SLOTS), in_specs=[v...]
  transfers between devices with their start and end apart: 2 -> 2, of which waited for: 0 -> 0; matrix products, arithmetic and copies ran while one was open for 0% -> 0% of each run, Pallas kernels for 38% -> 32%
where the time goes in v2:
time: 91.7 us; the launch traced here: 91.2 us
  Pallas kernels  50.1 us (55%)
  blocking collectives  27.9 us (30%)
  starting transfers between devices  13.2 us (14%)
    pallas_call x1, Pallas kernels, own_forces(): pl.pallas_call(own_kernel, out_shape=(f32(LEAVES, 4, SLOTS), i32(8, 2 * L...  29.3 us
    all_to_all x1, blocking collectives, on_device(): table = lax.all_to_all(sent, 'col', split_axis=0, concat_axis=0, tiled=True)  27.9 us
    pallas_call x1, Pallas kernels, near_forces(): pl.pallas_call(near_kernel, out_shape=f32(3, LEAVES * SLOTS), in_specs=[v...  18.9 us
    ppermute x1, starting transfers between devices, on_device(): after = lax.ppermute(table, 'row', down)  11.2 us
    pallas_call x1, Pallas kernels, pack(): pl.pallas_call(pack_kernel, out_shape=f32(LEAVES, 4, SLOTS), in_specs=[vm...  2 us
    ppermute x1, starting transfers between devices, on_device(): before = lax.ppermute(table, 'row', up)  1.92 us
  transfers between devices with their start and end apart: 2, of which 0 were waited for; matrix products, arithmetic and copies ran while one was open for 0% of the time, Pallas kernels for 32%

profile of v2, /device:TPU:1, one launch (start us, length us, event | category | flops | bytes accessed | tf_op | source)
XLA Modules:
  0.0 91.2 jit_solution(6154970848019439310)
XLA Ops:
  0.0 2.0 %pack.1 = f32[128,4,128]{2,1,0:T(4,128)} custom-call(f32[3,16384]{1,0:T(4,128)} %positions.1, f32[1,16384]{1,0:T(1,128)} %masses.1, s32[1,128]{1,0:T(1,128)} %counts.1), custom_call_target="tpu_custom_call" | custom-call | tf_op jit(solution)/shard_map/pack/pallas_call | solution.py:226
  2.0 0.0 copy-start
  2.0 27.9 %all_to_all.5.table = f32[128,4,128]{2,1,0:T(4,128)S(1)} all-to-all(f32[128,4,128]{2,1,0:T(4,128)} %pack.1), channel_id=1, replica_groups=mesh['row'=12,'col'=64] {'col'}, dimensions={0} | all-to-all | bytes 524288 | tf_op jit(solution)/shard_map/all_to_all | solution.py:264
  29.9 11.2 %collective-permute-start.1 = (f32[128,4,128]{2,1,0:T(4,128)S(1)}, f32[128,4,128]{2,1,0:T(4,128)S(1)}, u32[]{:S(2)}, u32[]{:S(2)}) collective-permute-start(f32[128,4,128]{2,1,0:T(4,128)S(1)} %all_to_all.5.table), channel_id=1, source_target_pairs={{64,0},{128,64},{192,128},{256,192},{320,256},{384,320},{448,384},... | collective-permute-start | bytes 786440 | tf_op jit(solution)/shard_map/ppermute | solution.py:269
  41.1 1.9 %collective-permute-start = (f32[128,4,128]{2,1,0:T(4,128)S(1)}, f32[128,4,128]{2,1,0:T(4,128)S(1)}, u32[]{:S(2)}, u32[]{:S(2)}) collective-permute-start(f32[128,4,128]{2,1,0:T(4,128)S(1)} %all_to_all.5.table), channel_id=1, source_target_pairs={{0,64},{64,128},{128,192},{192,256},{256,320},{320,384},{384,448},... | collective-permute-start | bytes 786440 | tf_op jit(solution)/shard_map/ppermute | solution.py:268
  43.0 0.0 copy-done
  43.1 29.3 %own_forces.1 = (f32[128,4,128]{2,1,0:T(4,128)S(1)}, s32[8,256]{1,0:T(8,128)S(1)}, s32[8,128]{1,0:T(8,128)S(1)}) custom-call(f32[128,4,128]{2,1,0:T(4,128)S(1)} %all_to_all.5.table, s32[8,128]{1,0:T(8,128)S(1)} %bitcast.1), custom_call_target="tpu_custom_call" | custom-call | flops 160000000 | tf_op jit(solution)/shard_map/own_forces/pallas_call | solution.py:236
  72.3 0.0 collective-permute-done.1.after
  72.3 0.0 collective-permute-done.before
  72.4 18.9 %near_forces.1 = f32[3,16384]{1,0:T(4,128)} custom-call(f32[128,4,128]{2,1,0:T(4,128)S(1)} %collective-permute-done.before, f32[128,4,128]{2,1,0:T(4,128)S(1)} %collective-permute-done.1.after, f32[128,4,128]{2,1,0:T(4,128)S(1)} %all_to_all.5.table, f32[128,4,128]{2,1,0:T(4,128)S(1)} %get-tuple-element.8.own_pull, s32[8,128]{1,0:T(8,128)S(1)} %bitcast.2, ...), custom_call_target="tpu_custom_call" | custom-call | flops 96000000 | tf_op jit(solution)/shard_map/near_forces/pallas_call | solution.py:249
Async XLA Ops:
  2.0 41.0 %copy-start = (s32[128,8]{0,1:T(8,128)S(1)}, s32[128,8]{0,1:T(8,128)}, u32[]{:S(2)}) copy-start(s32[128,8]{0,1:T(8,128)} %param.7) | copy-start | bytes 12292
  29.9 42.5 %collective-permute-start.1 = (f32[128,4,128]{2,1,0:T(4,128)S(1)}, f32[128,4,128]{2,1,0:T(4,128)S(1)}, u32[]{:S(2)}, u32[]{:S(2)}) collective-permute-start(f32[128,4,128]{2,1,0:T(4,128)S(1)} %all_to_all.5.table), channel_id=1, source_target_pairs={{64,0},{128,64},{192,128},{256,192},{320,256},{384,320},{448,384},... | collective-permute-start | bytes 786440 | tf_op jit(solution)/shard_map/ppermute | solution.py:269
  41.1 31.2 %collective-permute-start = (f32[128,4,128]{2,1,0:T(4,128)S(1)}, f32[128,4,128]{2,1,0:T(4,128)S(1)}, u32[]{:S(2)}, u32[]{:S(2)}) collective-permute-start(f32[128,4,128]{2,1,0:T(4,128)S(1)} %all_to_all.5.table), channel_id=1, source_target_pairs={{0,64},{64,128},{128,192},{192,256},{256,320},{320,384},{384,448},... | collective-permute-start | bytes 786440 | tf_op jit(solution)/shard_map/ppermute | solution.py:268

commit v3 on v2

--- a/solution.py
+++ b/solution.py
@@ -6,8 +6,11 @@
 from jax.sharding import PartitionSpec as P
 
 softening = 2.5e-07
-unit = 16
-blocks = 8
+unit = 32
+SHIFT = 3
+ROWS = 1 << SHIFT
+width = 8
+blocks = 12
 LEAVES = 128
 SLOTS = 128
 NEAR = 32
@@ -54,13 +57,15 @@
 
 
 def pair_forces(source_table, target_table, ids, spread, sums, chunks_vmem, chunks_smem, sem, leaves):
-    null_chunk = leaves * 8
+    per_leaf = SLOTS // ROWS
+    most = 8 * per_leaf
+    null_chunk = leaves * per_leaf
     ones = jnp.ones((8, SLOTS), jnp.bfloat16)
     live = (source_table[:, 3, :] >= 0.0).astype(jnp.float32).astype(jnp.bfloat16)
     if leaves < SLOTS:
         live = jnp.concatenate([live, jnp.zeros((SLOTS - leaves, SLOTS), jnp.bfloat16)], axis=0)
     count = lax.dot_general(ones, live, (((1,), (1,)), ((), ())), preferred_element_type=jnp.float32)
-    size = (count.astype(jnp.int32) + 15) >> 4
+    size = (count.astype(jnp.int32) + (ROWS - 1)) >> SHIFT
     mine = ids >= 0
     leaf = jnp.where(mine, ids, 0)
     size = jnp.where(mine, jnp.take_along_axis(size, leaf, axis=1), 0)
@@ -68,16 +73,17 @@
     starts, shifts, total = [], [], jnp.zeros((8, SLOTS), jnp.int32)
     for k in range(8):
         starts.append(total)
-        shifts.append(jnp.broadcast_to(leaf[k : k + 1, :], (8, SLOTS)) * 8 - total)
+        shifts.append(jnp.broadcast_to(leaf[k : k + 1, :], (8, SLOTS)) * per_leaf - total)
         total = total + jnp.broadcast_to(size[k : k + 1, :], (8, SLOTS))
-    for part in range(8):
+    for part in range(per_leaf):
         at = sub + 8 * part
         chunk = at + shifts[0]
         for k in range(1, 8):
             chunk = jnp.where(at >= starts[k], at + shifts[k], chunk)
-        chunks_vmem[8 * part : 8 * part + 8, :] = jnp.where(at < total, chunk, null_chunk)
-    chunks_vmem[64:72, :] = total
-    chunks_vmem[72:80, :] = jnp.full((8, SLOTS), null_chunk, jnp.int32)
+        chunks_vmem[pl.ds(1024 * part, 1024)] = jnp.where(at < total, chunk, null_chunk).reshape(1024)
+    target_of = lax.broadcasted_iota(jnp.int32, (8, SLOTS), 1)
+    chunks_vmem[pl.ds(SLOTS * most, 1024)] = (total * SLOTS + target_of).reshape(1024)
+    chunks_vmem[pl.ds(SLOTS * most + 1024, 1024)] = jnp.full((1024,), null_chunk, jnp.int32)
     to_scalars = pltpu.make_async_copy(chunks_vmem, chunks_smem, sem)
     to_scalars.start()
 
@@ -100,14 +106,13 @@
             tile = source_table[first * unit + u]
             tile = jnp.where(value == 3, jnp.maximum(tile, 0.0), tile)
             lhs.append(jnp.transpose(limbs_of(tile)).astype(jnp.bfloat16))
-        at = pl.multiple_of(first * (unit * SLOTS), unit * SLOTS)
-        spread[pl.ds(at, unit * SLOTS), :] = jnp.dot(
-            jnp.concatenate(lhs, axis=0), gather, preferred_element_type=jnp.float32
-        )
+        copied = jnp.dot(jnp.concatenate(lhs, axis=0), gather, preferred_element_type=jnp.float32)
+        pieces = unit * SLOTS // ROWS
+        spread[pl.ds(first * pieces, pieces)] = copied.reshape(pieces, ROWS, 4 * SLOTS)
         return 0
 
     lax.fori_loop(0, leaves // unit, spread_leaf, 0)
-    spread[leaves * SLOTS : leaves * SLOTS + 16, :] = jnp.zeros((16, 4 * SLOTS), jnp.float32)
+    spread[null_chunk] = jnp.zeros((ROWS, 4 * SLOTS), jnp.float32)
 
     def clear(i, _):
         for part in range(8):
@@ -120,35 +125,37 @@
     def pull_on(target, chunks):
         centre = [jnp.broadcast_to(target_table[target, c : c + 1, :], (8, SLOTS)) for c in range(3)]
         pulls = None
-        for u in range(8):
-            block = chunks[u // 2] + u % 2
-            rows = pl.ds(pl.multiple_of(block * 8, 8), 8)
-            delta = [spread[rows, SLOTS * c : SLOTS * c + SLOTS] - centre[c] for c in range(3)]
-            squares = [d * d for d in delta]
-            r = lax.rsqrt((squares[0] + softening) + (squares[1] + squares[2]))
-            weight = (spread[rows, 3 * SLOTS : 4 * SLOTS] * r) * (r * r)
-            parts = [weight * d for d in delta]
-            pulls = parts if pulls is None else [a + b for a, b in zip(pulls, parts)]
+        for chunk in chunks:
+            for row in range(0, ROWS, 8):
+                piece = [spread[chunk, row : row + 8, SLOTS * c : SLOTS * c + SLOTS] for c in range(4)]
+                delta = [piece[c] - centre[c] for c in range(3)]
+                squares = [d * d for d in delta]
+                r = lax.rsqrt((squares[0] + softening) + (squares[1] + squares[2]))
+                weight = (piece[3] * r) * (r * r)
+                parts = [weight * d for d in delta]
+                pulls = parts if pulls is None else [a + b for a, b in zip(pulls, parts)]
         for c in range(3):
             sums[target, 8 * c : 8 * c + 8, :] += pulls[c]
 
-    def chunks_at(target, at):
-        return tuple(chunks_smem[at + i, target] * 2 for i in range(4))
+    def chunks_at(at):
+        return tuple(chunks_smem[at + i * SLOTS] for i in range(width))
+
+    finished = SLOTS * most + 1024 + LEAVES - 1
 
     def body(state):
         target, at, chunks = state
         for _ in range(blocks):
             pull_on(target, chunks)
-            at = at + 4
-            done = at >= chunks_smem[64, target]
+            at = at + width * SLOTS
+            done = at >= chunks_smem[SLOTS * most + target]
             over = done & (target == LEAVES - 1)
             target = jnp.where(done & ~over, target + 1, target)
-            at = jnp.where(over, 72, jnp.where(done, 0, at))
-            chunks = chunks_at(target, at)
+            at = jnp.where(over, finished, jnp.where(done, target, at))
+            chunks = chunks_at(at)
         return target, at, chunks
 
     zero = jnp.int32(0)
-    lax.while_loop(lambda s: s[1] < 72, body, (zero, zero, chunks_at(zero, zero)))
+    lax.while_loop(lambda s: s[1] < finished, body, (zero, zero, chunks_at(zero)))
 
 
 def own_kernel(table, sources, out, slot_of, picked, spread, sums, chunks_vmem, chunks_smem, sem):
@@ -210,10 +217,10 @@
 
 def pair_scratch(leaves):
     return [
-        pltpu.VMEM((leaves * SLOTS + 16, 4 * SLOTS), jnp.float32),
+        pltpu.VMEM((leaves * (SLOTS // ROWS) + 1, ROWS, 4 * SLOTS), jnp.float32),
         pltpu.VMEM((LEAVES, 24, SLOTS), jnp.float32),
-        pltpu.VMEM((80, SLOTS), jnp.int32),
-        pltpu.SMEM((80, SLOTS), jnp.int32),
+        pltpu.VMEM((8 * SLOTS * SLOTS // ROWS + 2048,), jnp.int32),
+        pltpu.SMEM((8 * SLOTS * SLOTS // ROWS + 2048,), jnp.int32),
         pltpu.SemaphoreType.DMA,
     ]
 
@@ -225,7 +232,7 @@
 def pack(positions, masses, counts):
     return pl.pallas_call(
         pack_kernel,
-        out_shape=f32(LEAVES, 4, SLOTS),
+        out_shape=pltpu.VMEM((LEAVES, 4, SLOTS), jnp.float32),
         in_specs=[vmem, vmem, smem],
         out_specs=vmem,
         name="pack",

time: 91.7 us -> 85 us (0.927)
  Pallas kernels: 50.1 us -> 43.7 us
  blocking collectives: 27.9 us -> 26.9 us
    pallas_call x1, Pallas kernels: 29.3 us -> 24.8 us  [own_forces(): pl.pallas_call(own_kernel, out_shape=(f32(LEAVES, 4, SLOTS), i32(8, 2 * L...]
    pallas_call x1, Pallas kernels: 18.9 us -> 17.6 us  [near_forces(): pl.pallas_call(near_kernel, out_shape=f32(3, LEAVES * SLOTS), in_specs=[v...]
    all_to_all x1, blocking collectives: 27.9 us -> 26.9 us  [on_device(): table = lax.all_to_all(sent, 'col', split_axis=0, concat_axis=0, tiled=True)]
  transfers between devices with their start and end apart: 2 -> 2, of which waited for: 0 -> 0; matrix products, arithmetic and copies ran while one was open for 0% -> 0% of each run, Pallas kernels for 32% -> 29%
where the time goes in v3:
time: 85 us; the launch traced here: 84.5 us
  Pallas kernels  43.7 us (51%)
  blocking collectives  26.9 us (32%)
  starting transfers between devices  13.8 us (16%)
    all_to_all x1, blocking collectives, on_device(): table = lax.all_to_all(sent, 'col', split_axis=0, concat_axis=0, tiled=True)  26.9 us
    pallas_call x1, Pallas kernels, own_forces(): pl.pallas_call(own_kernel, out_shape=(f32(LEAVES, 4, SLOTS), i32(8, 2 * L...  24.8 us
    pallas_call x1, Pallas kernels, near_forces(): pl.pallas_call(near_kernel, out_shape=f32(3, LEAVES * SLOTS), in_specs=[v...  17.6 us
    ppermute x1, starting transfers between devices, on_device(): after = lax.ppermute(table, 'row', down)  11.9 us
    ppermute x1, starting transfers between devices, on_device(): before = lax.ppermute(table, 'row', up)  1.92 us
  transfers between devices with their start and end apart: 2, of which 0 were waited for; matrix products, arithmetic and copies ran while one was open for 0% of the time, Pallas kernels for 29%

profile of v3, /device:TPU:1, one launch (start us, length us, event | category | flops | bytes accessed | tf_op | source)
XLA Modules:
  0.0 84.5 jit_solution(9390334984370090108)
XLA Ops:
  0.0 1.3 %pack.1 = f32[128,4,128]{2,1,0:T(4,128)S(1)} custom-call(f32[3,16384]{1,0:T(4,128)} %positions.1, f32[1,16384]{1,0:T(1,128)} %masses.1, s32[1,128]{1,0:T(1,128)} %counts.1), custom_call_target="tpu_custom_call" | custom-call | tf_op jit(solution)/shard_map/pack/pallas_call | solution.py:233
  1.3 0.0 copy-start
  1.3 26.9 %all_to_all.5.table = f32[128,4,128]{2,1,0:T(4,128)S(1)} all-to-all(f32[128,4,128]{2,1,0:T(4,128)S(1)} %pack.1), channel_id=1, replica_groups=mesh['row'=12,'col'=64] {'col'}, dimensions={0} | all-to-all | bytes 524288 | tf_op jit(solution)/shard_map/all_to_all | solution.py:271
  28.2 11.9 %collective-permute-start.1 = (f32[128,4,128]{2,1,0:T(4,128)S(1)}, f32[128,4,128]{2,1,0:T(4,128)S(1)}, u32[]{:S(2)}, u32[]{:S(2)}) collective-permute-start(f32[128,4,128]{2,1,0:T(4,128)S(1)} %all_to_all.5.table), channel_id=1, source_target_pairs={{64,0},{128,64},{192,128},{256,192},{320,256},{384,320},{448,384},... | collective-permute-start | bytes 786440 | tf_op jit(solution)/shard_map/ppermute | solution.py:276
  40.1 1.9 %collective-permute-start = (f32[128,4,128]{2,1,0:T(4,128)S(1)}, f32[128,4,128]{2,1,0:T(4,128)S(1)}, u32[]{:S(2)}, u32[]{:S(2)}) collective-permute-start(f32[128,4,128]{2,1,0:T(4,128)S(1)} %all_to_all.5.table), channel_id=1, source_target_pairs={{0,64},{64,128},{128,192},{192,256},{256,320},{320,384},{384,448},... | collective-permute-start | bytes 786440 | tf_op jit(solution)/shard_map/ppermute | solution.py:275
  42.0 0.0 copy-done
  42.0 24.8 %own_forces.1 = (f32[128,4,128]{2,1,0:T(4,128)S(1)}, s32[8,256]{1,0:T(8,128)S(1)}, s32[8,128]{1,0:T(8,128)S(1)}) custom-call(f32[128,4,128]{2,1,0:T(4,128)S(1)} %all_to_all.5.table, s32[8,128]{1,0:T(8,128)S(1)} %bitcast.1), custom_call_target="tpu_custom_call" | custom-call | flops 160000000 | tf_op jit(solution)/shard_map/own_forces/pallas_call | solution.py:243
  66.9 0.0 collective-permute-done.1.after
  66.9 0.0 collective-permute-done.before
  66.9 17.6 %near_forces.1 = f32[3,16384]{1,0:T(4,128)} custom-call(f32[128,4,128]{2,1,0:T(4,128)S(1)} %collective-permute-done.before, f32[128,4,128]{2,1,0:T(4,128)S(1)} %collective-permute-done.1.after, f32[128,4,128]{2,1,0:T(4,128)S(1)} %all_to_all.5.table, f32[128,4,128]{2,1,0:T(4,128)S(1)} %get-tuple-element.8.own_pull, s32[8,128]{1,0:T(8,128)S(1)} %bitcast.2, ...), custom_call_target="tpu_custom_call" | custom-call | flops 96000000 | tf_op jit(solution)/shard_map/near_forces/pallas_call | solution.py:256
Async XLA Ops:
  1.3 40.7 %copy-start = (s32[128,8]{0,1:T(8,128)S(1)}, s32[128,8]{0,1:T(8,128)}, u32[]{:S(2)}) copy-start(s32[128,8]{0,1:T(8,128)} %param.7) | copy-start | bytes 12292
  28.2 38.7 %collective-permute-start.1 = (f32[128,4,128]{2,1,0:T(4,128)S(1)}, f32[128,4,128]{2,1,0:T(4,128)S(1)}, u32[]{:S(2)}, u32[]{:S(2)}) collective-permute-start(f32[128,4,128]{2,1,0:T(4,128)S(1)} %all_to_all.5.table), channel_id=1, source_target_pairs={{64,0},{128,64},{192,128},{256,192},{320,256},{384,320},{448,384},... | collective-permute-start | bytes 786440 | tf_op jit(solution)/shard_map/ppermute | solution.py:276
  40.1 26.8 %collective-permute-start = (f32[128,4,128]{2,1,0:T(4,128)S(1)}, f32[128,4,128]{2,1,0:T(4,128)S(1)}, u32[]{:S(2)}, u32[]{:S(2)}) collective-permute-start(f32[128,4,128]{2,1,0:T(4,128)S(1)} %all_to_all.5.table), channel_id=1, source_target_pairs={{0,64},{64,128},{128,192},{192,256},{256,320},{320,384},{384,448},... | collective-permute-start | bytes 786440 | tf_op jit(solution)/shard_map/ppermute | solution.py:275

commit v4 on v3

--- a/solution.py
+++ b/solution.py
@@ -6,11 +6,10 @@
 from jax.sharding import PartitionSpec as P
 
 softening = 2.5e-07
-unit = 32
 SHIFT = 3
 ROWS = 1 << SHIFT
 width = 8
-blocks = 12
+blocks = 20
 LEAVES = 128
 SLOTS = 128
 NEAR = 32
@@ -56,6 +55,15 @@
     picked[...] = lax.dot_general(leaf, chosen, lanes, preferred_element_type=jnp.float32).astype(jnp.int32)
 
 
+def clear_sums(sums):
+    def clear(i, _):
+        for part in range(8):
+            sums[i * 8 + part] = jnp.zeros((24, SLOTS), jnp.float32)
+        return 0
+
+    lax.fori_loop(0, LEAVES // 8, clear, 0)
+
+
 def pair_forces(source_table, target_table, ids, spread, sums, chunks_vmem, chunks_smem, sem, leaves):
     per_leaf = SLOTS // ROWS
     most = 8 * per_leaf
@@ -75,18 +83,28 @@
         starts.append(total)
         shifts.append(jnp.broadcast_to(leaf[k : k + 1, :], (8, SLOTS)) * per_leaf - total)
         total = total + jnp.broadcast_to(size[k : k + 1, :], (8, SLOTS))
-    for part in range(per_leaf):
-        at = sub + 8 * part
-        chunk = at + shifts[0]
-        for k in range(1, 8):
-            chunk = jnp.where(at >= starts[k], at + shifts[k], chunk)
-        chunks_vmem[pl.ds(1024 * part, 1024)] = jnp.where(at < total, chunk, null_chunk).reshape(1024)
+    groups = most // width
+    rows = groups + 8
     target_of = lax.broadcasted_iota(jnp.int32, (8, SLOTS), 1)
-    chunks_vmem[pl.ds(SLOTS * most, 1024)] = (total * SLOTS + target_of).reshape(1024)
-    chunks_vmem[pl.ds(SLOTS * most + 1024, 1024)] = jnp.full((1024,), null_chunk, jnp.int32)
+    finished = groups * SLOTS + LEAVES - 1
+    for i in range(width):
+        for part in range(rows // 8):
+            at = (sub + 8 * part) * width + i
+            chunk = at + shifts[0]
+            for k in range(1, 8):
+                chunk = jnp.where(at >= starts[k], at + shifts[k], chunk)
+            first = (i * rows + 8 * part) * SLOTS
+            chunks_vmem[pl.ds(first, 1024)] = jnp.where(at < total, chunk, null_chunk).reshape(1024)
+    for part in range(rows // 8):
+        group = sub + (8 * part + 1)
+        following = jnp.where(target_of == LEAVES - 1, finished, target_of + 1)
+        following = jnp.where(group * width < total, group * SLOTS + target_of, following)
+        following = jnp.where(group > groups, finished, following)
+        chunks_vmem[pl.ds((width * rows + 8 * part) * SLOTS, 1024)] = following.reshape(1024)
     to_scalars = pltpu.make_async_copy(chunks_vmem, chunks_smem, sem)
     to_scalars.start()
 
+    unit = leaves // 2
     limb = lax.broadcasted_iota(jnp.int32, (16, 4 * SLOTS), 0)
     column = lax.broadcasted_iota(jnp.int32, (16, 4 * SLOTS), 1)
     gather = ((limb < 12) & ((limb & 3) == column // SLOTS)).astype(jnp.float32).astype(jnp.bfloat16)
@@ -114,12 +132,6 @@
     lax.fori_loop(0, leaves // unit, spread_leaf, 0)
     spread[null_chunk] = jnp.zeros((ROWS, 4 * SLOTS), jnp.float32)
 
-    def clear(i, _):
-        for part in range(8):
-            sums[i * 8 + part] = jnp.zeros((24, SLOTS), jnp.float32)
-        return 0
-
-    lax.fori_loop(0, LEAVES // 8, clear, 0)
     to_scalars.wait()
 
     def pull_on(target, chunks):
@@ -138,29 +150,24 @@
             sums[target, 8 * c : 8 * c + 8, :] += pulls[c]
 
     def chunks_at(at):
-        return tuple(chunks_smem[at + i * SLOTS] for i in range(width))
-
-    finished = SLOTS * most + 1024 + LEAVES - 1
+        return tuple(chunks_smem[at + i * rows * SLOTS] for i in range(width))
 
     def body(state):
-        target, at, chunks = state
+        at, chunks = state
         for _ in range(blocks):
-            pull_on(target, chunks)
-            at = at + width * SLOTS
-            done = at >= chunks_smem[SLOTS * most + target]
-            over = done & (target == LEAVES - 1)
-            target = jnp.where(done & ~over, target + 1, target)
-            at = jnp.where(over, finished, jnp.where(done, target, at))
+            pull_on(at & (LEAVES - 1), chunks)
+            at = chunks_smem[at + width * rows * SLOTS]
             chunks = chunks_at(at)
-        return target, at, chunks
+        return at, chunks
 
     zero = jnp.int32(0)
-    lax.while_loop(lambda s: s[1] < finished, body, (zero, zero, chunks_at(zero)))
+    lax.while_loop(lambda s: s[0] < finished, body, (zero, chunks_at(zero)))
 
 
 def own_kernel(table, sources, out, slot_of, picked, spread, sums, chunks_vmem, chunks_smem, sem):
     ids = sources[...]
     ids = jnp.where(ids < LEAVES, ids, -1)
+    clear_sums(sums)
     number_neighbours(sources, slot_of, picked)
     pair_forces(table, table, ids, spread, sums, chunks_vmem, chunks_smem, sem, LEAVES)
 
@@ -174,7 +181,12 @@
     lax.fori_loop(0, LEAVES // 8, finish, 0)
 
 
-def near_kernel(before, after, table, own_pull, sources, slot_of, picked, out, leaves, spread, sums, chunks_vmem, chunks_smem, sem):
+def near_kernel(before, after, table, own_pull, sources, slot_of, picked_vmem, out, picked, picked_sem, leaves, spread, sums, chunks_vmem, chunks_smem, sem):
+    to_scalars = pltpu.make_async_copy(picked_vmem, picked, picked_sem)
+    to_scalars.start()
+    clear_sums(sums)
+    to_scalars.wait()
+
     def gather(i, _):
         for part in range(8):
             s = i * 8 + part
@@ -216,11 +228,12 @@
 
 
 def pair_scratch(leaves):
+    list_words = (width + 1) * (8 * SLOTS // ROWS // width + 8) * SLOTS
     return [
         pltpu.VMEM((leaves * (SLOTS // ROWS) + 1, ROWS, 4 * SLOTS), jnp.float32),
         pltpu.VMEM((LEAVES, 24, SLOTS), jnp.float32),
-        pltpu.VMEM((8 * SLOTS * SLOTS // ROWS + 2048,), jnp.int32),
-        pltpu.SMEM((8 * SLOTS * SLOTS // ROWS + 2048,), jnp.int32),
+        pltpu.VMEM((list_words,), jnp.int32),
+        pltpu.SMEM((list_words,), jnp.int32),
         pltpu.SemaphoreType.DMA,
     ]
 
@@ -256,9 +269,14 @@
     return pl.pallas_call(
         near_kernel,
         out_shape=f32(3, LEAVES * SLOTS),
-        in_specs=[vmem, vmem, vmem, vmem, vmem, vmem, smem],
+        in_specs=[vmem, vmem, vmem, vmem, vmem, vmem, vmem],
         out_specs=vmem,
-        scratch_shapes=[pltpu.VMEM((2 * NEAR, 4, SLOTS), jnp.float32)] + pair_scratch(2 * NEAR),
+        scratch_shapes=[
+            pltpu.SMEM((8, SLOTS), jnp.int32),
+            pltpu.SemaphoreType.DMA,
+            pltpu.VMEM((2 * NEAR, 4, SLOTS), jnp.float32),
+            *pair_scratch(2 * NEAR),
+        ],
         compiler_params=pltpu.CompilerParams(vmem_limit_bytes=30 * MIB),
         cost_estimate=cost(12),
         name="near_forces",

time: 85 us -> 83.8 us (0.986)
    pallas_call x1, Pallas kernels: 17.6 us -> 16.2 us  [near_forces(): pl.pallas_call(near_kernel, out_shape=f32(3, LEAVES * SLOTS), in_specs=[v...]
  transfers between devices with their start and end apart: 2 -> 2, of which waited for: 0 -> 0; matrix products, arithmetic and copies ran while one was open for 0% -> 0% of each run, Pallas kernels for 29% -> 30%
where the time goes in v4:
time: 83.8 us
  Pallas kernels  43 us (51%)
  blocking collectives  26.9 us (32%)
  starting transfers between devices  13.8 us (16%)
    all_to_all x1, blocking collectives, on_device(): table = lax.all_to_all(sent, 'col', split_axis=0, concat_axis=0, tiled=True)  26.9 us
    pallas_call x1, Pallas kernels, own_forces(): pl.pallas_call(own_kernel, out_shape=(f32(LEAVES, 4, SLOTS), i32(8, 2 * L...  25.5 us
    pallas_call x1, Pallas kernels, near_forces(): pl.pallas_call(near_kernel, out_shape=f32(3, LEAVES * SLOTS), in_specs=[v...  16.2 us
    ppermute x1, starting transfers between devices, on_device(): after = lax.ppermute(table, 'row', down)  11.9 us
    ppermute x1, starting transfers between devices, on_device(): before = lax.ppermute(table, 'row', up)  1.92 us
  transfers between devices with their start and end apart: 2, of which 0 were waited for; matrix products, arithmetic and copies ran while one was open for 0% of the time, Pallas kernels for 30%

profile of v4, /device:TPU:1, one launch (start us, length us, event | category | flops | bytes accessed | tf_op | source)
XLA Modules:
  0.0 83.8 jit_solution(534958993004809857)
XLA Ops:
  0.0 1.3 %pack.1 = f32[128,4,128]{2,1,0:T(4,128)S(1)} custom-call(f32[3,16384]{1,0:T(4,128)} %positions.1, f32[1,16384]{1,0:T(1,128)} %masses.1, s32[1,128]{1,0:T(1,128)} %counts.1), custom_call_target="tpu_custom_call" | custom-call | tf_op jit(solution)/shard_map/pack/pallas_call | solution.py:246
  1.3 0.0 copy-start
  1.3 26.9 %all_to_all.5.table = f32[128,4,128]{2,1,0:T(4,128)S(1)} all-to-all(f32[128,4,128]{2,1,0:T(4,128)S(1)} %pack.1), channel_id=1, replica_groups=mesh['row'=12,'col'=64] {'col'}, dimensions={0} | all-to-all | bytes 524288 | tf_op jit(solution)/shard_map/all_to_all | solution.py:289
  28.2 11.9 %collective-permute-start.1 = (f32[128,4,128]{2,1,0:T(4,128)S(1)}, f32[128,4,128]{2,1,0:T(4,128)S(1)}, u32[]{:S(2)}, u32[]{:S(2)}) collective-permute-start(f32[128,4,128]{2,1,0:T(4,128)S(1)} %all_to_all.5.table), channel_id=1, source_target_pairs={{64,0},{128,64},{192,128},{256,192},{320,256},{384,320},{448,384},... | collective-permute-start | bytes 786440 | tf_op jit(solution)/shard_map/ppermute | solution.py:294
  40.1 1.9 %collective-permute-start = (f32[128,4,128]{2,1,0:T(4,128)S(1)}, f32[128,4,128]{2,1,0:T(4,128)S(1)}, u32[]{:S(2)}, u32[]{:S(2)}) collective-permute-start(f32[128,4,128]{2,1,0:T(4,128)S(1)} %all_to_all.5.table), channel_id=1, source_target_pairs={{0,64},{64,128},{128,192},{192,256},{256,320},{320,384},{384,448},... | collective-permute-start | bytes 786440 | tf_op jit(solution)/shard_map/ppermute | solution.py:293
  42.0 0.0 copy-done
  42.0 25.5 %own_forces.1 = (f32[128,4,128]{2,1,0:T(4,128)S(1)}, s32[8,256]{1,0:T(8,128)S(1)}, s32[8,128]{1,0:T(8,128)S(1)}) custom-call(f32[128,4,128]{2,1,0:T(4,128)S(1)} %all_to_all.5.table, s32[8,128]{1,0:T(8,128)S(1)} %bitcast.1), custom_call_target="tpu_custom_call" | custom-call | flops 160000000 | tf_op jit(solution)/shard_map/own_forces/pallas_call | solution.py:256
  67.6 0.0 collective-permute-done.1.after
  67.6 0.0 collective-permute-done.before
  67.6 16.2 %near_forces.1 = f32[3,16384]{1,0:T(4,128)} custom-call(f32[128,4,128]{2,1,0:T(4,128)S(1)} %collective-permute-done.before, f32[128,4,128]{2,1,0:T(4,128)S(1)} %collective-permute-done.1.after, f32[128,4,128]{2,1,0:T(4,128)S(1)} %all_to_all.5.table, f32[128,4,128]{2,1,0:T(4,128)S(1)} %get-tuple-element.8.own_pull, s32[8,128]{1,0:T(8,128)S(1)} %bitcast.2, ...), custom_call_target="tpu_custom_call" | custom-call | flops 96000000 | tf_op jit(solution)/shard_map/near_forces/pallas_call | solution.py:269
Async XLA Ops:
  1.3 40.7 %copy-start = (s32[128,8]{0,1:T(8,128)S(1)}, s32[128,8]{0,1:T(8,128)}, u32[]{:S(2)}) copy-start(s32[128,8]{0,1:T(8,128)} %param.7) | copy-start | bytes 12292
  28.2 39.4 %collective-permute-start.1 = (f32[128,4,128]{2,1,0:T(4,128)S(1)}, f32[128,4,128]{2,1,0:T(4,128)S(1)}, u32[]{:S(2)}, u32[]{:S(2)}) collective-permute-start(f32[128,4,128]{2,1,0:T(4,128)S(1)} %all_to_all.5.table), channel_id=1, source_target_pairs={{64,0},{128,64},{192,128},{256,192},{320,256},{384,320},{448,384},... | collective-permute-start | bytes 786440 | tf_op jit(solution)/shard_map/ppermute | solution.py:294
  40.1 27.5 %collective-permute-start = (f32[128,4,128]{2,1,0:T(4,128)S(1)}, f32[128,4,128]{2,1,0:T(4,128)S(1)}, u32[]{:S(2)}, u32[]{:S(2)}) collective-permute-start(f32[128,4,128]{2,1,0:T(4,128)S(1)} %all_to_all.5.table), channel_id=1, source_target_pairs={{0,64},{64,128},{128,192},{192,256},{256,320},{320,384},{384,448},... | collective-permute-start | bytes 786440 | tf_op jit(solution)/shard_map/ppermute | solution.py:293

commit v5 on v4

--- a/solution.py
+++ b/solution.py
@@ -9,7 +9,6 @@
 SHIFT = 3
 ROWS = 1 << SHIFT
 width = 8
-blocks = 20
 LEAVES = 128
 SLOTS = 128
 NEAR = 32
@@ -154,7 +153,7 @@
 
     def body(state):
         at, chunks = state
-        for _ in range(blocks):
+        for _ in range(32 if leaves == LEAVES else 20):
             pull_on(at & (LEAVES - 1), chunks)
             at = chunks_smem[at + width * rows * SLOTS]
             chunks = chunks_at(at)

time: 83.8 us -> 83.1 us (level)
    pallas_call x1, Pallas kernels: 25.5 us -> 24.3 us  [own_forces(): pl.pallas_call(own_kernel, out_shape=(f32(LEAVES, 4, SLOTS), i32(8, 2 * L...]
  transfers between devices with their start and end apart: 2 -> 2, of which waited for: 0 -> 0; matrix products, arithmetic and copies ran while one was open for 0% -> 0% of each run, Pallas kernels for 30% -> 29%
where the time goes in v5:
time: 83.1 us; the launch traced here: 83.4 us
  Pallas kernels  42.7 us (51%)
  blocking collectives  26.9 us (32%)
  starting transfers between devices  13.8 us (17%)
    all_to_all x1, blocking collectives, on_device(): table = lax.all_to_all(sent, 'col', split_axis=0, concat_axis=0, tiled=True)  26.9 us
    pallas_call x1, Pallas kernels, own_forces(): pl.pallas_call(own_kernel, out_shape=(f32(LEAVES, 4, SLOTS), i32(8, 2 * L...  24.3 us
    pallas_call x1, Pallas kernels, near_forces(): pl.pallas_call(near_kernel, out_shape=f32(3, LEAVES * SLOTS), in_specs=[v...  17 us
    ppermute x1, starting transfers between devices, on_device(): after = lax.ppermute(table, 'row', down)  11.9 us
    ppermute x1, starting transfers between devices, on_device(): before = lax.ppermute(table, 'row', up)  1.92 us
  transfers between devices with their start and end apart: 2, of which 0 were waited for; matrix products, arithmetic and copies ran while one was open for 0% of the time, Pallas kernels for 29%

profile of v5, /device:TPU:1, one launch (start us, length us, event | category | flops | bytes accessed | tf_op | source)
XLA Modules:
  0.0 83.4 jit_solution(2645638664682054599)
XLA Ops:
  0.0 1.3 %pack.1 = f32[128,4,128]{2,1,0:T(4,128)S(1)} custom-call(f32[3,16384]{1,0:T(4,128)} %positions.1, f32[1,16384]{1,0:T(1,128)} %masses.1, s32[1,128]{1,0:T(1,128)} %counts.1), custom_call_target="tpu_custom_call" | custom-call | tf_op jit(solution)/shard_map/pack/pallas_call | solution.py:245
  1.3 0.0 copy-start
  1.3 26.9 %all_to_all.5.table = f32[128,4,128]{2,1,0:T(4,128)S(1)} all-to-all(f32[128,4,128]{2,1,0:T(4,128)S(1)} %pack.1), channel_id=1, replica_groups=mesh['row'=12,'col'=64] {'col'}, dimensions={0} | all-to-all | bytes 524288 | tf_op jit(solution)/shard_map/all_to_all | solution.py:288
  28.2 11.9 %collective-permute-start.1 = (f32[128,4,128]{2,1,0:T(4,128)S(1)}, f32[128,4,128]{2,1,0:T(4,128)S(1)}, u32[]{:S(2)}, u32[]{:S(2)}) collective-permute-start(f32[128,4,128]{2,1,0:T(4,128)S(1)} %all_to_all.5.table), channel_id=1, source_target_pairs={{64,0},{128,64},{192,128},{256,192},{320,256},{384,320},{448,384},... | collective-permute-start | bytes 786440 | tf_op jit(solution)/shard_map/ppermute | solution.py:293
  40.1 1.9 %collective-permute-start = (f32[128,4,128]{2,1,0:T(4,128)S(1)}, f32[128,4,128]{2,1,0:T(4,128)S(1)}, u32[]{:S(2)}, u32[]{:S(2)}) collective-permute-start(f32[128,4,128]{2,1,0:T(4,128)S(1)} %all_to_all.5.table), channel_id=1, source_target_pairs={{0,64},{64,128},{128,192},{192,256},{256,320},{320,384},{384,448},... | collective-permute-start | bytes 786440 | tf_op jit(solution)/shard_map/ppermute | solution.py:292
  42.0 0.0 copy-done
  42.0 24.3 %own_forces.1 = (f32[128,4,128]{2,1,0:T(4,128)S(1)}, s32[8,256]{1,0:T(8,128)S(1)}, s32[8,128]{1,0:T(8,128)S(1)}) custom-call(f32[128,4,128]{2,1,0:T(4,128)S(1)} %all_to_all.5.table, s32[8,128]{1,0:T(8,128)S(1)} %bitcast.1), custom_call_target="tpu_custom_call" | custom-call | flops 160000000 | tf_op jit(solution)/shard_map/own_forces/pallas_call | solution.py:255
  66.4 0.0 collective-permute-done.1.after
  66.4 0.0 collective-permute-done.before
  66.4 17.0 %near_forces.1 = f32[3,16384]{1,0:T(4,128)} custom-call(f32[128,4,128]{2,1,0:T(4,128)S(1)} %collective-permute-done.before, f32[128,4,128]{2,1,0:T(4,128)S(1)} %collective-permute-done.1.after, f32[128,4,128]{2,1,0:T(4,128)S(1)} %all_to_all.5.table, f32[128,4,128]{2,1,0:T(4,128)S(1)} %get-tuple-element.8.own_pull, s32[8,128]{1,0:T(8,128)S(1)} %bitcast.2, ...), custom_call_target="tpu_custom_call" | custom-call | flops 96000000 | tf_op jit(solution)/shard_map/near_forces/pallas_call | solution.py:268
Async XLA Ops:
  1.3 40.7 %copy-start = (s32[128,8]{0,1:T(8,128)S(1)}, s32[128,8]{0,1:T(8,128)}, u32[]{:S(2)}) copy-start(s32[128,8]{0,1:T(8,128)} %param.7) | copy-start | bytes 12292
  28.2 38.2 %collective-permute-start.1 = (f32[128,4,128]{2,1,0:T(4,128)S(1)}, f32[128,4,128]{2,1,0:T(4,128)S(1)}, u32[]{:S(2)}, u32[]{:S(2)}) collective-permute-start(f32[128,4,128]{2,1,0:T(4,128)S(1)} %all_to_all.5.table), channel_id=1, source_target_pairs={{64,0},{128,64},{192,128},{256,192},{320,256},{384,320},{448,384},... | collective-permute-start | bytes 786440 | tf_op jit(solution)/shard_map/ppermute | solution.py:293
  40.1 26.3 %collective-permute-start = (f32[128,4,128]{2,1,0:T(4,128)S(1)}, f32[128,4,128]{2,1,0:T(4,128)S(1)}, u32[]{:S(2)}, u32[]{:S(2)}) collective-permute-start(f32[128,4,128]{2,1,0:T(4,128)S(1)} %all_to_all.5.table), channel_id=1, source_target_pairs={{0,64},{64,128},{128,192},{192,256},{256,320},{320,384},{384,448},... | collective-permute-start | bytes 786440 | tf_op jit(solution)/shard_map/ppermute | solution.py:292
